TPU v7x, 32 devices: a whole 2x2x4 slice. The times are simulated.
32 devices in a mesh: ka: 8 (over z, core), band: 4 (over y, x).
Axes of the slice: x: 2, y: 2, z: 4, core: 2. Of those that a mesh axis runs over, the one named last changes fastest.
Arguments:
- occ_rows: bfloat16 [8, 2048, 128], P('ka', 'band'), may hold values from -0.5 to 0.5
- vir_rows: bfloat16 [8, 2048, 896], P('ka', 'band'), may hold values from -0.1875 to 0.1875
- trial_vectors: float32 [8, 2, 128, 896], P('ka', None, None, 'band'), may hold values from -6 to 6
- occ_energy: float32 [8, 128], P('ka'), may hold values from -1.2 to -0.3
- vir_energy: float32 [8, 896], P('ka', 'band'), may hold values from 0.1 to 1.5
- coulomb: bfloat16 [2048, 2048], P('band'), may hold values from -0.09375 to 0.09375
- exch_kernel: bfloat16 [8, 2048, 2048], P(None, 'band'), as said below
- minus_table: int32 [8, 8], replicated, may hold values from 0 to 7, as said below
Outputs:
- sigma_vectors: float32 [8, 2, 128, 896], P('ka', None, None, 'band')
Inputs may be any that keep to these rules, and one draw needn't show every extreme that they name: minus_table[k, q] is the k-point k - q on a group of 8 k-points: every row and every column holds each index once, and one q gives minus_table[k, q] == k for every k. Each exch_kernel[q] is symmetric.
All inputs are finite; a program needn't handle non-finite values.
Results may differ from a plain program's by a relative error of at most 0.0051.
Values may be sent and summed in bfloat16 or wider, within the bound.
A program may use at most 128 MiB of HBM per device.

v0:
```python
import functools

import jax
import jax.numpy as jnp
from jax import lax
from jax.experimental import pallas as pl
from jax.experimental.pallas import tpu as pltpu
from jax.sharding import PartitionSpec as P

F32 = jnp.float32
BF16 = jnp.bfloat16
CHUNK = 16


def dot_nt(left, right, **options):
    return lax.dot_general(
        left, right, (((1,), (1,)), ((), ())), preferred_element_type=F32, **options
    )


def kernel(
    kpoints,
    bands,
    vectors,
    occ,
    vir,
    trial,
    coulomb,
    exch,
    table,
    out,
    occ_full,
    occ_tile,
    trial_full,
    vir_turned,
    half_own,
    half_all,
    dens_all,
    dens_band,
    coulomb_here,
    exch_tile,
    pairs,
    screened,
    sums_send,
    sums_part,
    sums_recv,
    sigma_send,
    sigma_recv,
    local_sem,
    occ_band_sem,
    trial_sem,
    occ_point_sem,
    occ_pass_sem,
    half_sem,
    dens_sem,
    dens_band_sem,
    part_sem,
    sums_sem,
    sigma_sem,
):
    me = lax.axis_index("ka")
    band = lax.axis_index("band")
    groups = kpoints // 2
    group = lax.div(me, 2)
    core = lax.rem(me, 2)
    sibling = me + 1 - 2 * core
    rows, occupied = occ.shape
    auxiliary = occ_full.shape[0]
    half = rows // 2
    width = auxiliary // groups
    columns = trial.shape[1]
    piece = rows // groups
    scattered = piece % 128 == 0

    def tile_of(k):
        return lax.rem(k, 2) * groups + lax.div(k, 2)

    own_columns = pl.ds(pl.multiple_of(band * columns, columns), columns)

    def remote(source, target, sems, slot, device, send_slot=None):
        return pltpu.make_async_remote_copy(
            src_ref=source,
            dst_ref=target,
            send_sem=sems.at[0, slot if send_slot is None else send_slot],
            recv_sem=sems.at[1, slot],
            device_id=device,
            device_id_type=pl.DeviceIdType.MESH,
        )

    blocks = bands if scattered else 1
    block = width // blocks
    exch_copies = []
    for part in range(blocks):
        first = part * rows + group * piece if scattered else group * width
        copy = pltpu.make_async_copy(
            exch.at[
                :,
                pl.ds(pl.multiple_of(core * half, half), half),
                pl.ds(pl.multiple_of(first, 128), block),
            ],
            exch_tile.at[:, :, pl.ds(part * block, block)],
            local_sem.at[1 + part],
        )
        copy.start()
        exch_copies.append(copy)
    coulomb_copy = pltpu.make_async_copy(coulomb, coulomb_here, local_sem.at[0])
    coulomb_copy.start()

    trial_full[:, own_columns, :] = trial[...].astype(BF16)

    barrier = pltpu.get_barrier_semaphore()
    for step in range(1, bands):
        pl.semaphore_signal(
            barrier,
            inc=1,
            device_id=(me, lax.rem(band + step, bands)),
            device_id_type=pl.DeviceIdType.MESH,
        )
    for step in range(1, kpoints):
        pl.semaphore_signal(
            barrier,
            inc=1,
            device_id=(lax.rem(me + step, kpoints), band),
            device_id_type=pl.DeviceIdType.MESH,
        )
    pl.semaphore_wait(barrier, bands + kpoints - 2)

    own_rows = pl.ds(pl.multiple_of(band * rows, rows), rows)
    trial_copies = []
    for step in range(1, bands):
        copy = remote(
            trial_full.at[:, own_columns],
            trial_full.at[:, own_columns],
            trial_sem,
            step,
            (me, lax.rem(band + step, bands)),
        )
        copy.start()
        trial_copies.append(copy)
    occ_copies = []
    point_copies = []
    own_piece = pl.ds(pl.multiple_of(band * piece, piece), piece)
    mine = tile_of(me)
    if scattered:
        for step in range(1, groups):
            peer_group = lax.rem(group + step, groups)
            copy = remote(
                occ.at[pl.ds(pl.multiple_of(peer_group * piece, piece), piece)],
                occ_tile.at[mine, own_piece],
                occ_point_sem,
                step,
                (peer_group * 2 + core, band),
            )
            copy.start()
            point_copies.append(copy)
        occ_tile[mine, own_piece, :] = occ[
            pl.ds(pl.multiple_of(group * piece, piece), piece), :
        ]
        for copy in point_copies:
            copy.wait_recv()
        own_tiles = pl.ds(core * groups, groups)
        for step in range(1, bands):
            copy = remote(
                occ_tile.at[own_tiles, own_piece],
                occ_tile.at[own_tiles, own_piece],
                occ_band_sem,
                step,
                (me, lax.rem(band + step, bands)),
            )
            copy.start()
            occ_copies.append(copy)
    else:
        for step in range(1, bands):
            copy = remote(
                occ, occ_full.at[own_rows], occ_band_sem, step, (me, lax.rem(band + step, bands))
            )
            copy.start()
            occ_copies.append(copy)
        occ_full[own_rows, :] = occ[...]

    for copy in trial_copies:
        copy.wait_recv()
    for v in range(vectors):
        half_own[:, v * occupied : (v + 1) * occupied] = jnp.dot(
            vir[...], trial_full[v], preferred_element_type=F32
        ).astype(BF16)
    half_all[me] = half_own[pl.ds(pl.multiple_of(core * half, half), half), :]
    half_rows = [half_own.at[pl.ds(side * half, half)] for side in range(2)]
    signs = (1, -1)
    half_copies = [
        remote(
            half_own.at[pl.ds(pl.multiple_of((1 - core) * half, half), half)],
            half_all.at[me],
            half_sem,
            0,
            (sibling, band),
        )
    ]
    for way, sign in enumerate(signs):
        next_group = lax.rem(group + sign + groups, groups)
        for side in range(2):
            half_copies.append(
                remote(
                    half_rows[side],
                    half_all.at[me],
                    half_sem,
                    1 + 2 * way + core,
                    (next_group * 2 + side, band),
                    send_slot=1 + 2 * way + side,
                )
            )
    for copy in half_copies[1:] + half_copies[:1]:
        copy.start()

    def half_arrival(distance, way, owner_core):
        source = lax.rem(group - signs[way] * distance + groups, groups) * 2 + owner_core
        slot = (4 * (distance - 1) + 2 * way + owner_core) + 1
        return source, slot

    ones = jnp.ones((8, occupied), F32)
    occ_wide = occ[...].astype(F32)
    line = lax.broadcasted_iota(jnp.int32, (8, rows), 0)
    density = jnp.zeros((8, rows), F32)
    for v in range(vectors):
        here = half_own[:, v * occupied : (v + 1) * occupied].astype(F32)
        summed = dot_nt(ones, occ_wide * here, precision=lax.Precision.HIGHEST)
        density = jnp.where(line == v, summed, density)
    dens_all[me] = density
    dens_copies = []
    for step in range(1, kpoints):
        copy = remote(
            dens_all.at[me],
            dens_all.at[me],
            dens_sem,
            step,
            (lax.rem(me + step, kpoints), band),
        )
        copy.start()
        dens_copies.append(copy)

    for copy in occ_copies:
        copy.wait_recv()
    if scattered:
        pass_copies = [
            remote(
                occ_tile.at[own_tiles],
                occ_tile.at[own_tiles],
                occ_pass_sem,
                0,
                (sibling, band),
            )
        ]
        pass_copies[0].start()
    else:
        for step in range(1, groups):
            peer_group = lax.rem(group + step, groups)
            copy = remote(
                occ_full.at[pl.ds(pl.multiple_of(peer_group * width, width), width)],
                occ_tile.at[mine],
                occ_point_sem,
                step,
                (peer_group * 2 + core, band),
            )
            copy.start()
            point_copies.append(copy)
        occ_tile[mine] = occ_full[pl.ds(pl.multiple_of(group * width, width), width), :]
        pass_copies = [
            remote(
                occ_full.at[pl.ds(pl.multiple_of(group * width, width), width)],
                occ_tile.at[mine],
                occ_pass_sem,
                0,
                (sibling, band),
            )
        ]
        pass_copies[0].start()


    for step in range(1, 1 if scattered else groups):
        point_copies[step - 1].wait_recv()
        source = lax.rem(group - step + groups, groups) * 2 + core
        copy = remote(
            occ_tile.at[tile_of(source)], occ_tile.at[tile_of(source)], occ_pass_sem, step, (sibling, band)
        )
        copy.start()
        pass_copies.append(copy)

    def make_pairs(source):
        for v in range(vectors):
            pairs[source * vectors + v] = dot_nt(
                half_all[source, :, v * occupied : (v + 1) * occupied], occ_tile[tile_of(source)]
            )

    arrived = [me, sibling]
    for distance in range(1, groups // 2 + 1):
        for way in range(2):
            for owner_core in range(2):
                if distance == groups // 2 and owner_core != way:
                    continue
                source, slot = half_arrival(distance, way, owner_core)
                here = half_all.at[source]
                remote(here, here, half_sem, slot, (sibling, band)).wait_recv()
                arrived.append(source)
                farther = distance + 1
                if farther < groups // 2 or (farther == groups // 2 and owner_core == way):
                    next_group = lax.rem(group + signs[way] + groups, groups)
                    copy = remote(
                        here, here, half_sem, slot + 4, (next_group * 2 + core, band)
                    )
                    copy.start()
                    half_copies.append(copy)
        if distance == 1:
            vir_turned[...] = vir[...].T
            for copy in dens_copies:
                copy.wait_recv()
            density = dens_all[0]
            for k in range(1, kpoints):
                density += dens_all[k]
            dens_band[band] = jnp.concatenate(
                [density, jnp.zeros_like(density)], axis=0
            ).astype(BF16)
            dens_band_copies = []
            for step in range(1, bands):
                copy = remote(
                    dens_band.at[band],
                    dens_band.at[band],
                    dens_band_sem,
                    step,
                    (me, lax.rem(band + step, bands)),
                )
                copy.start()
                dens_band_copies.append(copy)
            for copy in pass_copies:
                copy.wait_recv()
            for copy in exch_copies:
                copy.wait()
            there = half_all.at[sibling]
            remote(there, there, half_sem, 0, (sibling, band)).wait_recv()
            for source in arrived:
                make_pairs(source)
        else:
            for source in arrived:
                make_pairs(source)
        arrived = []

    def screen(target):
        sources = [table[target, q] * vectors for q in range(kpoints)]

        def add_rows(chunk, carry):
            here = pl.ds(pl.multiple_of(chunk * CHUNK, CHUNK), CHUNK)
            totals = [jnp.zeros((CHUNK, width), F32) for _ in range(vectors)]
            for q in range(kpoints):
                factor = exch_tile[q, here, :].astype(F32)
                for v in range(vectors):
                    totals[v] += pairs[sources[q] + v, here, :] * factor
            for v in range(vectors):
                screened[v, here, :] = totals[v].astype(BF16)
            return carry

        lax.fori_loop(0, half // CHUNK, add_rows, 0)
        return jnp.concatenate(
            [
                jnp.dot(screened[v], occ_tile[tile_of(target)], preferred_element_type=F32)
                for v in range(vectors)
            ],
            axis=1,
        )

    stages = []
    for distance in range(groups // 2, 0, -1):
        level = [
            (distance, way, target_core)
            for way in range(2)
            for target_core in range(2)
            if distance < groups // 2 or target_core == way
        ]
        stages += sorted(level, key=lambda stage: stage[1] == stage[2])
    sums_copies = []
    for slot, (distance, way, target_core) in enumerate(stages):
        sign = signs[way]
        target = lax.rem(group + sign * distance + groups, groups) * 2 + target_core
        total = screen(target)
        earlier = (distance + 1, way, target_core)
        if earlier in stages:
            before = stages.index(earlier)
            there = sums_part.at[before]
            remote(there, there, part_sem, before, (sibling, band)).wait_recv()
            total += sums_part[before].astype(F32)
        sums_send[slot] = total.astype(BF16)
        next_group = lax.rem(group + sign + groups, groups)
        if distance > 1:
            copy = remote(
                sums_send.at[slot],
                sums_part.at[slot],
                part_sem,
                slot,
                (next_group * 2 + core, band),
            )
        else:
            copy = remote(
                sums_send.at[slot],
                sums_recv.at[1 + way, core],
                sums_sem,
                2 + 2 * way + core,
                (next_group * 2 + target_core, band),
                send_slot=2 + 2 * way + target_core,
            )
        copy.start()
        sums_copies.append(copy)
    last = len(stages)
    sums_send[last] = screen(sibling).astype(BF16)
    copy = remote(
        sums_send.at[last],
        sums_recv.at[0, core],
        sums_sem,
        0,
        (sibling, band),
    )
    copy.start()
    sums_copies.append(copy)
    sums_recv[0, core] = screen(me).astype(BF16)

    for copy in dens_band_copies:
        copy.wait_recv()
    coulomb_copy.wait()
    potential = dot_nt(coulomb_here[:, :rows], dens_band[0])
    for part in range(1, bands):
        potential += dot_nt(coulomb_here[:, part * rows : (part + 1) * rows], dens_band[part])
    there = sums_recv.at[0, 1 - core]
    remote(there, there, sums_sem, 0, (sibling, band)).wait_recv()
    for way in range(2):
        for side in range(2):
            there = sums_recv.at[1 + way, side]
            remote(there, there, sums_sem, 2 + 2 * way + side, (sibling, band)).wait_recv()
    coupling = []
    for v in range(vectors):
        pieces = []
        for side in range(2):
            part = slice(v * occupied, (v + 1) * occupied)
            total = sums_recv[0, side, :, part].astype(F32)
            for way in range(2):
                total += sums_recv[1 + way, side, :, part].astype(F32)
            lines = slice(side * half, (side + 1) * half)
            pieces.append(2.0 * potential[lines, v : v + 1] * occ_wide[lines] - total)
        coupling.append(jnp.concatenate(pieces, axis=0).astype(BF16))
    coupling = jnp.concatenate(coupling, axis=1)

    def sigma_of(peer):
        peer_columns = pl.ds(pl.multiple_of(peer * columns, columns), columns)
        return jnp.dot(vir_turned[peer_columns, :], coupling, preferred_element_type=F32)

    sigma_copies = []
    for step in range(1, bands):
        peer = lax.rem(band + step, bands)
        sigma_send[step] = sigma_of(peer).astype(BF16)
        copy = remote(sigma_send.at[step], sigma_recv.at[step], sigma_sem, step, (me, peer))
        copy.start()
        sigma_copies.append(copy)
    result = sigma_of(band)
    for step in range(1, bands):
        sigma_copies[step - 1].wait_recv()
        result += sigma_recv[step].astype(F32)
    for v in range(vectors):
        out[v] = result[:, v * occupied : (v + 1) * occupied]

    for copy in (
        trial_copies
        + occ_copies
        + half_copies
        + point_copies
        + pass_copies
        + dens_copies
        + dens_band_copies
        + sigma_copies
        + sums_copies
    ):
        copy.wait_send()


def coupled_part(kpoints, bands, occ, vir, trial, coulomb, exch, table, vectors):
    rows, occupied = occ.shape
    columns = trial.shape[1]
    merged = vectors * occupied
    auxiliary = coulomb.shape[1]
    half = rows // 2
    width = auxiliary * 2 // kpoints
    vmem = pl.BlockSpec(memory_space=pltpu.VMEM)
    hbm = pl.BlockSpec(memory_space=pl.ANY)
    smem = pl.BlockSpec(memory_space=pltpu.SMEM)
    both = pltpu.SemaphoreType.DMA
    return pl.pallas_call(
        functools.partial(kernel, kpoints, bands, vectors),
        out_shape=jax.ShapeDtypeStruct(trial.shape, F32),
        in_specs=[vmem, vmem, vmem, hbm, hbm, smem],
        out_specs=vmem,
        scratch_shapes=[
            pltpu.VMEM((auxiliary, occupied), BF16),
            pltpu.VMEM((kpoints, width, occupied), BF16),
            pltpu.VMEM((vectors, bands * columns, occupied), BF16),
            pltpu.VMEM((bands * columns, rows), BF16),
            pltpu.VMEM((rows, merged), BF16),
            pltpu.VMEM((kpoints, half, merged), BF16),
            pltpu.VMEM((kpoints, 8, rows), F32),
            pltpu.VMEM((bands, 16, rows), BF16),
            pltpu.VMEM((rows, auxiliary), BF16),
            pltpu.VMEM((kpoints, half, width), BF16),
            pltpu.VMEM((kpoints * vectors, half, width), F32),
            pltpu.VMEM((vectors, half, width), BF16),
            pltpu.VMEM((kpoints, half, merged), BF16),
            pltpu.VMEM((kpoints, half, merged), BF16),
            pltpu.VMEM((3, 2, half, merged), BF16),
            pltpu.VMEM((bands, columns, merged), BF16),
            pltpu.VMEM((bands, columns, merged), BF16),
            both((1 + bands,)),
            both((2, bands)),
            both((2, bands)),
            both((2, kpoints)),
            both((2, kpoints)),
            both((2, kpoints * 2)),
            both((2, kpoints)),
            both((2, bands)),
            both((2, kpoints)),
            both((2, kpoints)),
            both((2, bands)),
        ],
        compiler_params=pltpu.CompilerParams(
            collective_id=0, has_side_effects=True, vmem_limit_bytes=60 * 2**20
        ),
        name="coupled",
    )(occ, vir, trial, coulomb, exch, table)


def per_device(
    occ_rows, vir_rows, trial_vectors, occ_energy, vir_energy, coulomb, exch_kernel, minus_table
):
    kpoints = lax.axis_size("ka")
    bands = lax.axis_size("band")
    vectors = trial_vectors.shape[1]
    trial_turned = jnp.swapaxes(trial_vectors[0], 1, 2)
    coupled = coupled_part(
        kpoints,
        bands,
        occ_rows[0],
        vir_rows[0],
        trial_turned,
        coulomb,
        exch_kernel,
        minus_table,
        vectors,
    )
    energy_gaps = vir_energy[0][:, None] - occ_energy[0][None, :]
    return jnp.swapaxes(energy_gaps[None] * trial_turned + coupled, 1, 2)[None]


def solution(mesh):
    in_specs = (
        P("ka", "band", None),
        P("ka", "band", None),
        P("ka", None, None, "band"),
        P("ka", None),
        P("ka", "band"),
        P("band", None),
        P(None, "band", None),
        P(),
    )
    out_specs = P("ka", None, None, "band")
    return jax.shard_map(
        per_device, mesh=mesh, in_specs=in_specs, out_specs=out_specs, check_vma=False
    )
```

profile of v0, /device:TPU:0, one launch (start us, length us, event | category | flops | bytes accessed | tf_op | source)
XLA Modules:
  0.0 67.1 jit_solution(1218864177674911831)
XLA Ops:
  0.0 0.0 copy-start
  0.0 0.8 %broadcast_subtract_fusion = f32[224,128]{1,0:T(8,128)S(1)} fusion(f32[128]{0:T(128)} %bitcast.16, f32[224]{0:T(256)} %bitcast.15), kind=kLoop, calls=%fused_computation.1 | loop fusion | flops 28672 | bytes 116096 | tf_op jit(solution)/shard_map/sub | solution.py:551
  0.8 64.6 %coupled.1 = f32[2,224,128]{2,1,0:T(8,128)} custom-call(bf16[512,128]{1,0:T(8,128)(2,1)} %bitcast.14, bf16[512,896]{1,0:T(8,128)(2,1)} %bitcast.13, f32[2,224,128]{2,1,0:T(8,128)} %bitcast.12, bf16[512,2048]{1,0:T(8,128)(2,1)} %coulomb.1, bf16[8,512,2048]{2,1,0:T(8,128)(2,1)} %exch.1, s32[8,8]{1,0:T(8,128)} %table.1), custom_call_target="tpu_custom_call" | custom-call | tf_op jit(solution)/shard_map/coupled/pallas_call | solution.py:491
  65.5 0.0 copy-done
  65.5 1.7 %add_bitcast_fusion = f32[1,2,128,224]{2,3,1,0:T(8,128)} fusion(f32[2,224,128]{2,1,0:T(8,128)} %coupled.1, f32[224,128]{1,0:T(8,128)S(1)} %broadcast_subtract_fusion, f32[1,2,128,224]{2,3,1,0:T(8,128)S(1)} %copy-done), kind=kLoop, calls=%fused_computation | loop fusion | flops 114688 | bytes 802816 | tf_op jit(solution)/shard_map/broadcast_in_dim | solution.py:552
Async XLA Ops:
  0.0 65.5 %copy-start = (f32[1,2,128,224]{2,3,1,0:T(8,128)S(1)}, f32[1,2,128,224]{2,3,1,0:T(8,128)}, u32[]{:S(2)}) copy-start(f32[1,2,128,224]{2,3,1,0:T(8,128)} %param.10) | copy-start | bytes 688132
where the time goes:
time: 67.3 us; the launch traced here: 67.1 us
  Pallas kernels  64.6 us (96%)
  other arithmetic  2.48 us (4%)
    pallas_call x1, Pallas kernels, coupled_part(): pl.pallas_call(functools.partial(kernel, kpoints, bands, vectors), out_sh...  64.6 us
    broadcast_in_dim x1, other arithmetic, per_device(): return jnp.swapaxes(energy_gaps[None] * trial_turned + coupled, 1, 2)[None]  1.66 us

commit v1 on v0

v1 whole, which is shorter than its diff:
```python
import functools

import jax
import jax.numpy as jnp
from jax import lax
from jax.experimental import pallas as pl
from jax.experimental.pallas import tpu as pltpu
from jax.sharding import PartitionSpec as P

F32 = jnp.float32
BF16 = jnp.bfloat16
CHUNK = 16
SPAN = 512


def dot_nt(left, right, **options):
    return lax.dot_general(
        left, right, (((1,), (1,)), ((), ())), preferred_element_type=F32, **options
    )


def aligned(start, size):
    return pl.ds(pl.multiple_of(start, size), size)


def kernel(
    kpoints,
    bands,
    vectors,
    occ,
    vir,
    trial,
    coulomb,
    exch,
    table,
    out,
    trial_full,
    vir_turned,
    half_own,
    half_all,
    occ_tile,
    dens_all,
    dens_band,
    potential,
    coulomb_here,
    exch_tile,
    pairs,
    screened,
    sums_send,
    sums_slot,
    coupling,
    sigma_send,
    sigma_recv,
    local_sem,
    trial_sem,
    point_sem,
    occ_sem,
    occ_pass_sem,
    half_send_sem,
    half_recv_sem,
    half_pass_sem,
    dens_sem,
    dens_band_sem,
    sums_send_sem,
    sums_recv_sem,
    sigma_sem,
):
    me = lax.axis_index("ka")
    band = lax.axis_index("band")
    groups = kpoints // 2
    count = groups // 2
    group = lax.div(me, 2)
    core = lax.rem(me, 2)
    sibling = me + 1 - 2 * core
    pair = lax.div(group, 2)
    side = lax.rem(group, 2)
    partner = group + 1 - 2 * side
    rows, occupied = occ.shape
    columns = trial.shape[1]
    block = rows // groups
    piece = rows // 2
    width = bands * piece
    near_x = band + 1 - 2 * lax.rem(band, 2)
    near_y = lax.rem(band + 2, bands)
    corner = bands - 1 - band
    others = (corner, near_x, near_y)

    def tile_of(k):
        return lax.rem(k, 2) * groups + lax.div(k, 2)

    def remote(source, target, send, recv, device):
        return pltpu.make_async_remote_copy(
            src_ref=source,
            dst_ref=target,
            send_sem=send,
            recv_sem=recv,
            device_id=device,
            device_id_type=pl.DeviceIdType.MESH,
        )

    def arrival(target, recv):
        return remote(target, target, recv, recv, (sibling, band))

    exch_copies = []
    for part in range(bands):
        copy = pltpu.make_async_copy(
            exch.at[
                :,
                aligned((2 * pair + core) * block, block),
                aligned(part * rows + side * piece, piece),
            ],
            exch_tile.at[:, :, pl.ds(part * piece, piece)],
            local_sem.at[1 + part],
        )
        copy.start()
        exch_copies.append(copy)
    coulomb_copy = pltpu.make_async_copy(coulomb, coulomb_here, local_sem.at[0])
    coulomb_copy.start()

    own_columns = aligned(band * columns, columns)
    trial_full[:, own_columns, :] = trial[...].astype(BF16)

    barrier = pltpu.get_barrier_semaphore()
    for peer in others:
        pl.semaphore_signal(
            barrier, inc=1, device_id=(me, peer), device_id_type=pl.DeviceIdType.MESH
        )
    for step in range(1, kpoints):
        pl.semaphore_signal(
            barrier,
            inc=1,
            device_id=(lax.rem(me + step, kpoints), band),
            device_id_type=pl.DeviceIdType.MESH,
        )
    pl.semaphore_wait(barrier, len(others) + kpoints - 1)

    started = []

    def send(copy):
        copy.start()
        started.append(copy)
        return copy

    trial_copies = []
    for v in range(vectors):
        trial_copies.append(
            [
                send(
                    remote(
                        trial_full.at[v, own_columns],
                        trial_full.at[v, own_columns],
                        trial_sem.at[0, v, way],
                        trial_sem.at[1, v, way],
                        (me, peer),
                    )
                )
                for way, peer in enumerate(others)
            ]
        )

    def piece_of(owner):
        return aligned(owner * piece, piece)

    mine = tile_of(me)
    for step in range(1, groups):
        peer = lax.rem(group + step, groups)
        send(
            remote(
                occ.at[aligned(lax.rem(peer, 2) * piece, piece)],
                occ_tile.at[mine, piece_of(band)],
                point_sem.at[0, step],
                point_sem.at[1, group],
                (peer * 2 + core, band),
            )
        )
    occ_tile[mine, piece_of(band), :] = occ[aligned(side * piece, piece), :]

    def occ_out(source_group):
        tile = core * groups + source_group
        here = occ_tile.at[tile, piece_of(band)]
        for way, peer in ((1, near_x), (2, near_y)):
            send(
                remote(
                    here,
                    here,
                    occ_sem.at[0, source_group, way],
                    occ_sem.at[1, source_group, way],
                    (me, peer),
                )
            )
        occ_pass(source_group, 0, band)

    def occ_pass(source_group, way, owner):
        here = occ_tile.at[core * groups + source_group, piece_of(owner)]
        send(
            remote(
                here,
                here,
                occ_pass_sem.at[0, source_group, way],
                occ_pass_sem.at[1, source_group, way],
                (sibling, band),
            )
        )

    tile_order = [lax.rem(group + step, groups) for step in range(groups)]
    occ_out(tile_order[0])

    def own_half(v):
        for copy in trial_copies[v]:
            copy.wait_recv()
        half_own[v] = jnp.dot(vir[...], trial_full[v], preferred_element_type=F32).astype(BF16)
        lines = pl.ds(v * block, block)
        own_block = 2 * pair + core
        half_all[me, lines, :] = half_own[v, aligned(own_block * block, block), :]
        slot = 0
        destinations = []
        for step in range(1, count):
            other = lax.rem(pair + step, count)
            near = lax.select(other > pair, 2 * other, 2 * other + 1)
            destinations += [(2 * other + side_core, near * 2 + side_core) for side_core in range(2)]
        destinations += [(2 * pair + side_core, partner * 2 + side_core) for side_core in range(2)]
        destinations.append((2 * pair + 1 - core, sibling))
        for slot, (which, device) in enumerate(destinations):
            send(
                remote(
                    half_own.at[v, aligned(which * block, block)],
                    half_all.at[me, lines],
                    half_send_sem.at[v, slot],
                    half_recv_sem.at[v, me],
                    (device, band),
                )
            )

    for v in range(vectors):
        own_half(v)

    ones = jnp.ones((8, occupied), F32)
    occ_wide = occ[...].astype(F32)
    density = jnp.concatenate(
        [
            dot_nt(ones, occ_wide * half_own[v].astype(F32), precision=lax.Precision.HIGHEST)[:1]
            for v in range(vectors)
        ],
        axis=0,
    )
    dens_all[me] = density
    dens_copies = [
        send(
            remote(
                dens_all.at[me],
                dens_all.at[me],
                dens_sem.at[0, step],
                dens_sem.at[1, step],
                (lax.rem(me + step, kpoints), band),
            )
        )
        for step in range(1, kpoints)
    ]

    for source_group in tile_order[1:]:
        arrival(
            occ_tile.at[core * groups + source_group, piece_of(band)],
            point_sem.at[1, source_group],
        ).wait_recv()
        occ_out(source_group)

    vir_turned[...] = vir[...].T

    passes = []

    def take_halves(v, source_group, forward):
        for owner_core in range(2):
            source = source_group * 2 + owner_core
            here = half_all.at[source, pl.ds(v * block, block)]
            arrival(here, half_recv_sem.at[v, source]).wait_recv()
            if forward is None:
                continue
            copy = remote(
                here,
                here,
                half_pass_sem.at[v, source],
                half_recv_sem.at[v, source],
                (partner * 2 + core, band),
            )
            pl.when(forward == 1)(copy.start)
            passes.append((copy, forward))

    far_groups = []
    for step in range(groups - 2):
        low = lax.rem(2 * pair + 2 + step, groups)
        high = lax.rem(2 * pair + 2 * groups - 1 - step, groups)
        source_group = lax.select(2 * pair < count, low, high)
        forward = lax.select(source_group < 2 * pair, 1 - side, side)
        far_groups.append((source_group, forward))

    def take_all_halves(v):
        there = half_all.at[sibling, pl.ds(v * block, block)]
        arrival(there, half_recv_sem.at[v, sibling]).wait_recv()
        take_halves(v, partner, None)
        for source_group, forward in far_groups:
            take_halves(v, source_group, forward)

    def occ_in(position):
        source_group = tile_order[position]
        tile = core * groups + source_group
        first = position < groups // 2
        for way, peer, onward in ((1, near_x, near_y), (2, near_y, near_x)):
            here = occ_tile.at[tile, piece_of(peer)]
            arrival(here, occ_sem.at[1, source_group, way]).wait_recv()
            if first == (way == 1):
                send(
                    remote(
                        here,
                        here,
                        occ_sem.at[0, source_group, 3],
                        occ_sem.at[1, source_group, 3],
                        (me, onward),
                    )
                )
            occ_pass(source_group, way, peer)

    take_all_halves(0)
    for position in range(groups):
        occ_in(position)

    for copy in dens_copies:
        copy.wait_recv()
    density = dens_all[0]
    for k in range(1, kpoints):
        density += dens_all[k]
    dens_band[band] = density
    dens_band_copies = [
        send(
            remote(
                dens_band.at[band],
                dens_band.at[band],
                dens_band_sem.at[0, way],
                dens_band_sem.at[1, way],
                (me, peer),
            )
        )
        for way, peer in enumerate(others)
    ]
    for v in range(1, vectors):
        take_all_halves(v)
    for source_group in tile_order:
        here = occ_tile.at[core * groups + source_group, piece_of(corner)]
        arrival(here, occ_sem.at[1, source_group, 3]).wait_recv()
        occ_pass(source_group, 3, corner)
    for copy in exch_copies:
        copy.wait()

    def make_pairs(source):
        pairs[source] = dot_nt(half_all[source], occ_tile[tile_of(source)])

    for source_group in tile_order:
        make_pairs(source_group * 2 + core)

    for copy in dens_band_copies:
        copy.wait_recv()
    coulomb_copy.wait()
    spread = jnp.zeros((16 - vectors, rows), F32)
    total = jnp.zeros((rows, 16), F32)
    for part in range(bands):
        here = jnp.concatenate([dens_band[part], spread], axis=0).astype(BF16)
        total += dot_nt(coulomb_here[:, part * rows : (part + 1) * rows], here)
    potential[:, :16] = total

    for source_group in tile_order:
        tile = (1 - core) * groups + source_group
        for way, owner in enumerate((band, near_x, near_y, corner)):
            arrival(
                occ_tile.at[tile, piece_of(owner)], occ_pass_sem.at[1, source_group, way]
            ).wait_recv()
        make_pairs(source_group * 2 + 1 - core)

    def screen(v, targets):
        sources = [[table[target, q] for q in range(kpoints)] for target in targets]
        spans = width // SPAN

        def add_rows(index, carry):
            start = lax.div(index, spans) * CHUNK
            here = aligned(start, CHUNK)
            there = pl.ds(pl.multiple_of(v * block + start, CHUNK), CHUNK)
            across = aligned(lax.rem(index, spans) * SPAN, SPAN)
            totals = [jnp.zeros((CHUNK, SPAN), F32) for _ in targets]
            for q in range(kpoints):
                factor = exch_tile[q, here, across].astype(F32)
                for n in range(len(targets)):
                    totals[n] += pairs[sources[n][q], there, across] * factor
            for n in range(len(targets)):
                screened[n, here, across] = totals[n].astype(BF16)
            return carry

        lax.fori_loop(0, block // CHUNK * spans, add_rows, 0)
        return [
            jnp.dot(screened[n], occ_tile[tile_of(target)], preferred_element_type=F32)
            for n, target in enumerate(targets)
        ]

    own_block = 2 * pair + core
    lower = 2 * pair
    higher = groups - 2 - lower
    outward = lax.select(side == 0, higher, lower)

    def send_sums(v):
        for step in range(groups - 1):
            rising = lax.select(step <= higher, groups - 1 - step, step - higher - 1)
            falling = lax.select(step <= lower, step, groups + lower - step)
            target_group = lax.select(side == 0, rising, falling)
            through = step < outward
            gather = step > outward
            totals = screen(v, [target_group * 2 + n for n in range(2)])
            for n in range(2):
                target = target_group * 2 + n
                total = totals[n]
                sending = sums_send.at[v, step, n]
                slot = lax.select(
                    through,
                    2 * groups + target,
                    2 * own_block + lax.select(gather, jnp.int32(0), side),
                )
                device = lax.select(through, partner * 2 + core, target)

                @pl.when(gather)
                def _(total=total, target=target, sending=sending):
                    before = sums_slot.at[v, 2 * groups + target]
                    arrival(before, sums_recv_sem.at[v, 2 * groups + target]).wait_recv()
                    sending[...] = (total + before[...].astype(F32)).astype(BF16)

                @pl.when(jnp.logical_not(gather))
                def _(total=total, sending=sending):
                    sending[...] = total.astype(BF16)

                send(
                    remote(
                        sending,
                        sums_slot.at[v, slot],
                        sums_send_sem.at[v, step, n],
                        sums_recv_sem.at[v, slot],
                        (device, band),
                    )
                )
        totals = screen(v, [sibling, me])
        sending = sums_send.at[v, groups - 1, 0]
        sending[...] = totals[0].astype(BF16)
        slot = 2 * own_block + side
        send(
            remote(
                sending,
                sums_slot.at[v, slot],
                sums_send_sem.at[v, groups - 1, 0],
                sums_recv_sem.at[v, slot],
                (sibling, band),
            )
        )
        sums_slot[v, slot] = totals[1].astype(BF16)

    sigma_copies = []

    def sigma_of(v, peer):
        return jnp.dot(
            vir_turned[aligned(peer * columns, columns), :],
            coupling[v],
            preferred_element_type=F32,
        )

    def make_sigma(v):
        def take(slot):
            arrival(sums_slot.at[v, slot], sums_recv_sem.at[v, slot]).wait_recv()

        take(2 * (2 * pair + core) + 1 - side)
        for part in range(2):
            take(2 * (2 * pair + 1 - core) + part)
        for step in range(count):
            other = lax.rem(pair + step, count)
            for side_core in range(2):
                which = 2 * other + side_core
                if step:
                    take(2 * which)
                total = sums_slot[v, 2 * which].astype(F32)
                if not step:
                    total += sums_slot[v, 2 * which + 1].astype(F32)
                lines = aligned(which * block, block)
                direct = 2.0 * potential[lines, v : v + 1] * occ[lines, :].astype(F32)
                coupling[v, lines, :] = (direct - total).astype(BF16)
        copies = []
        for way, peer in enumerate(others):
            sigma_send[v, way] = sigma_of(v, peer).astype(BF16)
            copies.append(
                send(
                    remote(
                        sigma_send.at[v, way],
                        sigma_recv.at[v, way],
                        sigma_sem.at[0, v, way],
                        sigma_sem.at[1, v, way],
                        (me, peer),
                    )
                )
            )
        sigma_copies.append(copies)
        out[v] = sigma_of(v, band)

    for v in range(vectors):
        send_sums(v)
    for v in range(vectors):
        make_sigma(v)
    for v in range(vectors):
        result = out[v]
        for way, copy in enumerate(sigma_copies[v]):
            copy.wait_recv()
            result += sigma_recv[v, way].astype(F32)
        out[v] = result

    for copy in started:
        copy.wait_send()
    for copy, forward in passes:
        pl.when(forward == 1)(copy.wait_send)


def coupled_part(kpoints, bands, occ, vir, trial, coulomb, exch, table, vectors):
    rows, occupied = occ.shape
    columns = trial.shape[1]
    groups = kpoints // 2
    block = rows // groups
    width = bands * rows // 2
    vmem = pl.BlockSpec(memory_space=pltpu.VMEM)
    hbm = pl.BlockSpec(memory_space=pl.ANY)
    smem = pl.BlockSpec(memory_space=pltpu.SMEM)
    dma = pltpu.SemaphoreType.DMA
    return pl.pallas_call(
        functools.partial(kernel, kpoints, bands, vectors),
        out_shape=jax.ShapeDtypeStruct(trial.shape, F32),
        in_specs=[vmem, vmem, vmem, hbm, hbm, smem],
        out_specs=vmem,
        scratch_shapes=[
            pltpu.VMEM((vectors, bands * columns, occupied), BF16),
            pltpu.VMEM((bands * columns, rows), BF16),
            pltpu.VMEM((vectors, rows, occupied), BF16),
            pltpu.VMEM((kpoints, vectors * block, occupied), BF16),
            pltpu.VMEM((kpoints, width, occupied), BF16),
            pltpu.VMEM((kpoints, vectors, rows), F32),
            pltpu.VMEM((bands, vectors, rows), F32),
            pltpu.VMEM((rows, 128), F32),
            pltpu.VMEM(coulomb.shape, BF16),
            pltpu.VMEM((kpoints, block, width), BF16),
            pltpu.VMEM((kpoints, vectors * block, width), F32),
            pltpu.VMEM((2, block, width), BF16),
            pltpu.VMEM((vectors, groups, 2, block, occupied), BF16),
            pltpu.VMEM((vectors, 2 * groups + kpoints, block, occupied), BF16),
            pltpu.VMEM((vectors, rows, occupied), BF16),
            pltpu.VMEM((vectors, bands - 1, columns, occupied), BF16),
            pltpu.VMEM((vectors, bands - 1, columns, occupied), BF16),
            dma((1 + bands,)),
            dma((2, vectors, bands)),
            dma((2, groups)),
            dma((2, groups, bands)),
            dma((2, groups, bands)),
            dma((vectors, groups + 1)),
            dma((vectors, kpoints)),
            dma((vectors, kpoints)),
            dma((2, kpoints)),
            dma((2, bands)),
            dma((vectors, groups, 2)),
            dma((vectors, 2 * groups + kpoints)),
            dma((2, vectors, bands)),
        ],
        compiler_params=pltpu.CompilerParams(
            collective_id=0, has_side_effects=True, vmem_limit_bytes=60 * 2**20
        ),
        name="coupled",
    )(occ, vir, trial, coulomb, exch, table)


def per_device(
    occ_rows, vir_rows, trial_vectors, occ_energy, vir_energy, coulomb, exch_kernel, minus_table
):
    kpoints = lax.axis_size("ka")
    bands = lax.axis_size("band")
    vectors = trial_vectors.shape[1]
    trial_turned = jnp.swapaxes(trial_vectors[0], 1, 2)
    coupled = coupled_part(
        kpoints,
        bands,
        occ_rows[0],
        vir_rows[0],
        trial_turned,
        coulomb,
        exch_kernel,
        minus_table,
        vectors,
    )
    energy_gaps = vir_energy[0][:, None] - occ_energy[0][None, :]
    return jnp.swapaxes(energy_gaps[None] * trial_turned + coupled, 1, 2)[None]


def solution(mesh):
    in_specs = (
        P("ka", "band", None),
        P("ka", "band", None),
        P("ka", None, None, "band"),
        P("ka", None),
        P("ka", "band"),
        P("band", None),
        P(None, "band", None),
        P(),
    )
    out_specs = P("ka", None, None, "band")
    return jax.shard_map(
        per_device, mesh=mesh, in_specs=in_specs, out_specs=out_specs, check_vma=False
    )
```

time: 67.3 us -> 55.7 us (0.83)
  Pallas kernels: 64.6 us -> 53 us
    pallas_call x1, Pallas kernels: 64.6 us -> 53 us  [coupled_part(): pl.pallas_call(functools.partial(kernel, kpoints, bands, vectors), out_sh...]
where the time goes in v1:
time: 55.7 us; the launch traced here: 55.6 us
  Pallas kernels  53 us (95%)
  other arithmetic  2.48 us (4%)
    pallas_call x1, Pallas kernels, coupled_part(): pl.pallas_call(functools.partial(kernel, kpoints, bands, vectors), out_sh...  53 us
    broadcast_in_dim x1, other arithmetic, per_device(): return jnp.swapaxes(energy_gaps[None] * trial_turned + coupled, 1, 2)[None]  1.66 us

profile of v1, /device:TPU:0, one launch (start us, length us, event | category | flops | bytes accessed | tf_op | source)
XLA Modules:
  0.0 55.6 jit_solution(4195381822069044083)
XLA Ops:
  0.0 0.0 copy-start
  0.0 0.8 %broadcast_subtract_fusion = f32[224,128]{1,0:T(8,128)S(1)} fusion(f32[128]{0:T(128)} %bitcast.16, f32[224]{0:T(256)} %bitcast.15), kind=kLoop, calls=%fused_computation.1 | loop fusion | flops 28672 | bytes 116096 | tf_op jit(solution)/shard_map/sub | solution.py:593
  0.8 53.0 %coupled.1 = f32[2,224,128]{2,1,0:T(8,128)} custom-call(bf16[512,128]{1,0:T(8,128)(2,1)} %bitcast.14, bf16[512,896]{1,0:T(8,128)(2,1)} %bitcast.13, f32[2,224,128]{2,1,0:T(8,128)} %bitcast.12, bf16[512,2048]{1,0:T(8,128)(2,1)} %coulomb.1, bf16[8,512,2048]{2,1,0:T(8,128)(2,1)} %exch.1, s32[8,8]{1,0:T(8,128)} %table.1), custom_call_target="tpu_custom_call" | custom-call | tf_op jit(solution)/shard_map/coupled/pallas_call | solution.py:531
  53.9 0.0 copy-done
  53.9 1.7 %add_bitcast_fusion = f32[1,2,128,224]{2,3,1,0:T(8,128)} fusion(f32[2,224,128]{2,1,0:T(8,128)} %coupled.1, f32[224,128]{1,0:T(8,128)S(1)} %broadcast_subtract_fusion, f32[1,2,128,224]{2,3,1,0:T(8,128)S(1)} %copy-done), kind=kLoop, calls=%fused_computation | loop fusion | flops 114688 | bytes 802816 | tf_op jit(solution)/shard_map/broadcast_in_dim | solution.py:594
Async XLA Ops:
  0.0 53.9 %copy-start = (f32[1,2,128,224]{2,3,1,0:T(8,128)S(1)}, f32[1,2,128,224]{2,3,1,0:T(8,128)}, u32[]{:S(2)}) copy-start(f32[1,2,128,224]{2,3,1,0:T(8,128)} %param.10) | copy-start | bytes 688132

commit v2 on v1

v2 whole, which is shorter than its diff:
```python
import functools

import jax
import jax.numpy as jnp
from jax import lax
from jax.experimental import pallas as pl
from jax.experimental.pallas import tpu as pltpu
from jax.sharding import PartitionSpec as P

F32 = jnp.float32
BF16 = jnp.bfloat16
CHUNK = 16
SPAN = 512


def dot_nt(left, right, **options):
    return lax.dot_general(
        left, right, (((1,), (1,)), ((), ())), preferred_element_type=F32, **options
    )


def aligned(start, size):
    return pl.ds(pl.multiple_of(start, size), size)


def kernel(
    kpoints,
    bands,
    vectors,
    occ_given,
    vir_given,
    trial_given,
    occ_energy_given,
    vir_energy_given,
    coulomb,
    exch,
    table_given,
    out,
    occ,
    vir,
    trial,
    occ_energy,
    vir_energy,
    table,
    gaps,
    exch_wide,
    trial_full,
    vir_turned,
    half_own,
    half_all,
    occ_tile,
    dens_all,
    dens_band,
    potential,
    coulomb_here,
    exch_tile,
    pairs,
    held,
    sums_send,
    sums_slot,
    coupling,
    sigma_send,
    sigma_recv,
    local_sem,
    trial_sem,
    point_sem,
    occ_send_sem,
    occ_sem,
    occ_pass_sem,
    half_send_sem,
    half_recv_sem,
    half_pass_sem,
    dens_sem,
    dens_band_sem,
    sums_send_sem,
    sums_recv_sem,
    sigma_sem,
):
    me = lax.axis_index("ka")
    band = lax.axis_index("band")
    groups = kpoints // 2
    count = groups // 2
    group = lax.div(me, 2)
    core = lax.rem(me, 2)
    sibling = me + 1 - 2 * core
    pair = lax.div(group, 2)
    side = lax.rem(group, 2)
    partner = group + 1 - 2 * side
    rows, occupied = occ.shape
    columns = trial.shape[1]
    block = rows // groups
    piece = rows // 2
    width = bands * piece
    near_x = band + 1 - 2 * lax.rem(band, 2)
    near_y = lax.rem(band + 2, bands)
    corner = bands - 1 - band
    others = (corner, near_x, near_y)

    def tile_of(k):
        return lax.rem(k, 2) * groups + lax.div(k, 2)

    def remote(source, target, send, recv, device):
        return pltpu.make_async_remote_copy(
            src_ref=source,
            dst_ref=target,
            send_sem=send,
            recv_sem=recv,
            device_id=device,
            device_id_type=pl.DeviceIdType.MESH,
        )

    def arrival(target, recv):
        return remote(target, target, recv, recv, (sibling, band))

    def drain(held, sem):
        pltpu.make_async_copy(held, held, sem).wait()

    barrier = pltpu.get_barrier_semaphore()
    for peer in others:
        pl.semaphore_signal(
            barrier, inc=1, device_id=(me, peer), device_id_type=pl.DeviceIdType.MESH
        )
    for step in range(1, kpoints):
        pl.semaphore_signal(
            barrier,
            inc=1,
            device_id=(lax.rem(me + step, kpoints), band),
            device_id_type=pl.DeviceIdType.MESH,
        )

    load_copies = []
    for given, here in (
        (trial_given, trial),
        (occ_given, occ),
        (vir_given, vir),
        (table_given, table),
        (occ_energy_given, occ_energy),
        (vir_energy_given, vir_energy),
    ):
        copy = pltpu.make_async_copy(given, here, local_sem.at[2 + len(load_copies)])
        copy.start()
        load_copies.append(copy)
    trial_load, occ_load, vir_load, *other_loads = load_copies
    for part in range(bands):
        pltpu.make_async_copy(
            exch.at[
                :,
                aligned((2 * pair + core) * block, block),
                aligned(part * rows + side * piece, piece),
            ],
            exch_tile.at[:, :, pl.ds(part * piece, piece)],
            local_sem.at[1],
        ).start()
    coulomb_copy = pltpu.make_async_copy(coulomb, coulomb_here, local_sem.at[0])
    coulomb_copy.start()

    own_columns = aligned(band * columns, columns)
    trial_load.wait()
    trial_full[:, own_columns, :] = trial[...].astype(BF16)
    pl.semaphore_wait(barrier, len(others) + kpoints - 1)

    for v in range(vectors):
        for peer in others:
            remote(
                trial_full.at[v, own_columns],
                trial_full.at[v, own_columns],
                trial_sem.at[vectors],
                trial_sem.at[v],
                (me, peer),
            ).start()

    def piece_of(owner):
        return aligned(owner * piece, piece)

    far_groups = []
    for step in range(groups - 2):
        low = lax.rem(2 * pair + 2 + step, groups)
        high = lax.rem(2 * pair + 2 * groups - 1 - step, groups)
        far_groups.append(lax.select(2 * pair < count, low, high))
    order = [group, partner] + far_groups

    mine = tile_of(me)
    occ_load.wait()
    point_copies = []
    for step, peer in enumerate(order[1:]):
        copy = remote(
            occ.at[aligned(lax.rem(peer, 2) * piece, piece)],
            occ_tile.at[mine, piece_of(band)],
            point_sem.at[0, step],
            point_sem.at[1, group],
            (peer * 2 + core, band),
        )
        copy.start()
        point_copies.append(copy)
    occ_tile[mine, piece_of(band), :] = occ[aligned(side * piece, piece), :]

    def occ_out(source_group):
        tile = core * groups + source_group
        here = occ_tile.at[tile, piece_of(band)]
        for way, peer in ((1, near_x), (2, near_y)):
            remote(
                here,
                here,
                occ_send_sem.at[0],
                occ_sem.at[source_group, way - 1],
                (me, peer),
            ).start()
        occ_pass(source_group, 0, band).start()

    def occ_pass(source_group, way, owner):
        here = occ_tile.at[core * groups + source_group, piece_of(owner)]
        return remote(
            here,
            here,
            occ_pass_sem.at[0],
            occ_pass_sem.at[1 + way // (bands - 1)],
            (sibling, band),
        )

    occ_out(group)
    vir_load.wait()
    vir_turned[...] = vir[...].T
    for copy in other_loads:
        copy.wait()
    turned = jnp.broadcast_to(vir_energy[...], (occupied, columns)).T
    gaps[...] = turned - occ_energy[...]
    drain(exch_tile, local_sem.at[1])

    def widen(k, carry):
        exch_wide[k] = exch_tile[k].astype(F32)
        return carry

    lax.fori_loop(0, kpoints, widen, 0)

    def take_point(source_group):
        arrival(
            occ_tile.at[core * groups + source_group, piece_of(band)],
            point_sem.at[1, source_group],
        ).wait_recv()
        occ_out(source_group)

    def own_half(v):
        drain(sigma_recv.at[v], trial_sem.at[v])
        half_own[v] = jnp.dot(vir[...], trial_full[v], preferred_element_type=F32).astype(BF16)
        lines = pl.ds(v * block, block)
        own_block = 2 * pair + core
        half_all[me, lines, :] = half_own[v, aligned(own_block * block, block), :]
        destinations = []
        for step in range(1, count):
            other = lax.rem(pair + step, count)
            near = lax.select(other > pair, 2 * other, 2 * other + 1)
            destinations += [(2 * other + side_core, near * 2 + side_core) for side_core in range(2)]
        destinations += [(2 * pair + side_core, partner * 2 + side_core) for side_core in range(2)]
        destinations.append((2 * pair + 1 - core, sibling))
        for which, device in destinations:
            remote(
                half_own.at[v, aligned(which * block, block)],
                half_all.at[me, lines],
                half_send_sem.at[0],
                half_recv_sem.at[v, me],
                (device, band),
            ).start()

    take_point(partner)
    for v in range(vectors):
        own_half(v)

    for source_group in far_groups:
        take_point(source_group)

    def half_pass(v, position, owner_core):
        source = far_groups[position] * 2 + owner_core
        here = half_all.at[source, pl.ds(v * block, block)]
        return remote(
            here,
            here,
            half_pass_sem.at[v, position, owner_core],
            half_recv_sem.at[v, source],
            (partner * 2 + core, band),
        )

    def take_half(v, source):
        here = half_all.at[source, pl.ds(v * block, block)]
        arrival(here, half_recv_sem.at[v, source]).wait_recv()

    def passing(source_group):
        return lax.select(source_group < 2 * pair, 1 - side, side) == 1

    def take_far(v, position):
        for owner_core in range(2):
            take_half(v, far_groups[position] * 2 + owner_core)
            pl.when(passing(far_groups[position]))(half_pass(v, position, owner_core).start)

    def occ_turn(position):
        source_group = order[position]
        tile = core * groups + source_group
        if position < groups // 2:
            owner, onward = near_x, near_y
        else:
            owner, onward = near_y, near_x
        here = occ_tile.at[tile, piece_of(owner)]
        return remote(
            here,
            here,
            occ_send_sem.at[0],
            occ_sem.at[source_group, 2],
            (me, onward),
        )

    def occ_in(position):
        source_group = order[position]
        tile = core * groups + source_group
        for way, owner in ((1, near_x), (2, near_y)):
            here = occ_tile.at[tile, piece_of(owner)]
            arrival(here, occ_sem.at[source_group, way - 1]).wait_recv()
            if (position < groups // 2) == (way == 1):
                occ_turn(position).start()
            occ_pass(source_group, way, owner).start()

    inner = lax.select(2 * pair < count, side, 1 - side) == 1

    @pl.when(inner)
    def _():
        turns = [(v, far) for v in range(vectors) for far in range(groups - 2)]
        for position in range(max(groups, len(turns))):
            if position < groups:
                occ_in(position)
            if position < len(turns):
                take_far(*turns[position])

    @pl.when(jnp.logical_not(inner))
    def _():
        for position in range(groups):
            occ_in(position)

    ones = jnp.ones((8, occupied), F32)
    occ_wide = occ[...].astype(F32)
    dens_all[me] = jnp.concatenate(
        [
            dot_nt(ones, occ_wide * half_own[v].astype(F32), precision=lax.Precision.HIGHEST)[:1]
            for v in range(vectors)
        ],
        axis=0,
    )
    for step in range(1, kpoints):
        remote(
            dens_all.at[me],
            dens_all.at[me],
            dens_sem.at[0],
            dens_sem.at[1],
            (lax.rem(me + step, kpoints), band),
        ).start()

    def take_corner(position):
        source_group = order[position]
        here = occ_tile.at[core * groups + source_group, piece_of(corner)]
        arrival(here, occ_sem.at[source_group, 2]).wait_recv()
        occ_pass(source_group, bands - 1, corner).start()

    def take_halves(v):
        take_half(v, sibling)
        for source in (partner * 2, partner * 2 + 1):
            take_half(v, source)

        @pl.when(jnp.logical_not(inner))
        def _():
            for far in range(groups - 2):
                take_far(v, far)

    def make_pairs(v, owners):
        lines = pl.ds(v * block, block)
        for source in range(kpoints):
            tile = tile_of(source)
            if len(owners) == bands:
                pairs[source, lines] = dot_nt(half_all[source, lines], occ_tile[tile])
                continue
            for owner in owners:
                part = piece_of(owner)
                pairs[source, lines, part] = dot_nt(
                    half_all[source, lines], occ_tile[tile, part]
                )

    def sum_density():
        drain(dens_all.at[pl.ds(0, kpoints - 1)], dens_sem.at[1])
        density = dens_all[0]
        for k in range(1, kpoints):
            density += dens_all[k]
        dens_band[band] = density
        for peer in others:
            remote(
                dens_band.at[band],
                dens_band.at[band],
                dens_band_sem.at[0],
                dens_band_sem.at[1],
                (me, peer),
            ).start()

    def make_potential():
        drain(dens_band.at[pl.ds(0, bands - 1)], dens_band_sem.at[1])
        coulomb_copy.wait()
        spread = jnp.zeros((16 - vectors, rows), F32)
        total = jnp.zeros((rows, 16), F32)
        for part in range(bands):
            here = jnp.concatenate([dens_band[part], spread], axis=0).astype(BF16)
            total += dot_nt(coulomb_here[:, part * rows : (part + 1) * rows], here)
        potential[:, :16] = total

    def screen(v, targets, spans):
        sources = [[table[target, q] for q in range(kpoints)] for target in targets]
        results = [jnp.zeros((block, occupied), F32) for _ in targets]
        for across, span in spans:
            chunks = [[] for _ in targets]
            for start in range(0, block, CHUNK):
                totals = [jnp.zeros((CHUNK, span), F32) for _ in targets]
                for q in range(kpoints):
                    factor = exch_wide[q, pl.ds(start, CHUNK), across]
                    for n in range(len(targets)):
                        there = pl.ds(v * block + start, CHUNK)
                        totals[n] += pairs[sources[n][q], there, across] * factor
                for n in range(len(targets)):
                    chunks[n].append(totals[n].astype(BF16))
            for n, target in enumerate(targets):
                results[n] += jnp.dot(
                    jnp.concatenate(chunks[n], axis=0),
                    occ_tile[tile_of(target), across],
                    preferred_element_type=F32,
                )
        return results

    whole = [(pl.ds(first, SPAN), SPAN) for first in range(0, width, SPAN)]
    early = [(piece_of(owner), piece) for owner in (band, near_x, near_y)]
    late = [(piece_of(corner), piece)]

    own_block = 2 * pair + core
    lower = 2 * pair
    higher = groups - 2 - lower
    outward = lax.select(side == 0, higher, lower)

    def far_target(step):
        rising = lax.select(step <= higher, groups - 1 - step, step - higher - 1)
        falling = lax.select(step <= lower, step, groups + lower - step)
        return lax.select(side == 0, rising, falling)

    def sums_to(v, step, n, device, slot, recv):
        remote(
            sums_send.at[v, step, n],
            sums_slot.at[v, slot],
            sums_send_sem.at[v],
            sums_recv_sem.at[v, recv],
            (device, band),
        ).start()

    def screen_far(v, step, spans, before=None):
        target_group = far_target(step)
        totals = screen(v, [target_group * 2 + n for n in range(2)], spans)
        for n in range(2):
            held[v, step, n] = totals[n] if before is None else held[v, step, n] + totals[n]

    def send_far(v, step):
        target_group = far_target(step)
        through = step < outward

        @pl.when(step <= outward)
        def _():
            for n in range(2):
                target = target_group * 2 + n
                sums_send[v, step, n] = held[v, step, n].astype(BF16)
                sums_to(
                    v,
                    step,
                    n,
                    lax.select(through, partner * 2 + core, target),
                    lax.select(through, 2 * groups + target, 2 * own_block + side),
                    lax.select(through, target, kpoints),
                )

    def gather_far(v):
        for step in range(groups - 1):

            @pl.when(step > outward)
            def _(step=step):
                for n in range(2):
                    target = far_target(step) * 2 + n
                    before = sums_slot.at[v, 2 * groups + target]
                    arrival(before, sums_recv_sem.at[v, target]).wait_recv()
                    total = held[v, step, n] + before[...].astype(F32)
                    sums_send[v, step, n] = total.astype(BF16)
                    sums_to(v, step, n, target, 2 * own_block, kpoints)

    def send_own(v):
        totals = screen(v, [sibling, me], whole)
        sending = sums_send.at[v, groups - 1, 0]
        sending[...] = totals[0].astype(BF16)
        slot = 2 * own_block + side
        remote(
            sending,
            sums_slot.at[v, slot],
            sums_send_sem.at[v],
            sums_recv_sem.at[v, kpoints],
            (sibling, band),
        ).start()
        sums_slot[v, slot] = totals[1].astype(BF16)


    def sigma_of(v, peer):
        return jnp.dot(
            vir_turned[aligned(peer * columns, columns), :],
            coupling[v],
            preferred_element_type=F32,
        )

    def make_sigma(v):
        drain(sums_slot.at[v, pl.ds(0, 2 * count + 1)], sums_recv_sem.at[v, kpoints])
        for step in range(count):
            other = lax.rem(pair + step, count)
            for side_core in range(2):
                which = 2 * other + side_core
                total = sums_slot[v, 2 * which].astype(F32)
                if not step:
                    total += sums_slot[v, 2 * which + 1].astype(F32)
                lines = aligned(which * block, block)
                direct = 2.0 * potential[lines, v : v + 1] * occ[lines, :].astype(F32)
                coupling[v, lines, :] = (direct - total).astype(BF16)
        for way, peer in enumerate(others):
            sigma_send[v, way] = sigma_of(v, peer).astype(BF16)
            remote(
                sigma_send.at[v, way],
                sigma_recv.at[v, way],
                sigma_sem.at[vectors],
                sigma_sem.at[v],
                (me, peer),
            ).start()
        out[v] = gaps[...] * trial[v] + sigma_of(v, band)

    take_halves(0)
    for position in range(groups // 2):
        take_corner(position)
    drain(occ_tile.at[pl.ds(0, groups), pl.ds(0, width - piece)], occ_pass_sem.at[1])
    make_pairs(0, (band, near_x, near_y))
    screen_far(0, 0, early)
    for position in range(groups // 2, groups):
        take_corner(position)
    drain(occ_tile.at[pl.ds(0, groups), pl.ds(0, piece)], occ_pass_sem.at[2])
    make_pairs(0, (corner,))
    screen_far(0, 0, late, True)
    send_far(0, 0)
    for step in range(1, groups - 1):
        screen_far(0, step, whole)
        send_far(0, step)
    sum_density()
    for v in range(1, vectors):
        take_halves(v)
        make_pairs(v, (band, near_x, near_y, corner))
        for step in range(groups - 1):
            screen_far(v, step, whole)
            send_far(v, step)
        gather_far(v - 1)
    send_own(0)
    make_potential()
    gather_far(vectors - 1)
    make_sigma(0)
    for v in range(1, vectors):
        send_own(v)
        make_sigma(v)
    for v in range(vectors):
        drain(sigma_recv.at[v], sigma_sem.at[v])
        result = out[v]
        for way in range(bands - 1):
            result += sigma_recv[v, way].astype(F32)
        out[v] = result

    drain(sigma_send, trial_sem.at[vectors])
    drain(sigma_send, sigma_sem.at[vectors])
    for copy in point_copies:
        copy.wait_send()
    drain(occ_tile.at[pl.ds(0, groups), pl.ds(0, width - piece)], occ_send_sem.at[0])
    drain(occ_tile.at[pl.ds(0, groups)], occ_pass_sem.at[0])
    drain(half_all.at[pl.ds(0, groups + 1)], half_send_sem.at[0])
    drain(dens_all.at[pl.ds(0, kpoints - 1)], dens_sem.at[0])
    drain(dens_band.at[pl.ds(0, bands - 1)], dens_band_sem.at[0])
    for v in range(vectors):
        drain(sums_slot.at[v, pl.ds(0, 2 * groups - 1)], sums_send_sem.at[v])
        for far in range(groups - 2):
            for owner_core in range(2):
                pl.when(passing(far_groups[far]))(half_pass(v, far, owner_core).wait_send)


def coupled_part(
    kpoints, bands, occ, vir, trial, occ_energy, vir_energy, coulomb, exch, table
):
    rows, occupied = occ.shape
    vectors, columns = trial.shape[:2]
    groups = kpoints // 2
    block = rows // groups
    width = bands * rows // 2
    vmem = pl.BlockSpec(memory_space=pltpu.VMEM)
    hbm = pl.BlockSpec(memory_space=pltpu.HBM)
    dma = pltpu.SemaphoreType.DMA
    return pl.pallas_call(
        functools.partial(kernel, kpoints, bands, vectors),
        out_shape=jax.ShapeDtypeStruct(trial.shape, F32),
        in_specs=[hbm] * 8,
        out_specs=vmem,
        scratch_shapes=[
            pltpu.VMEM(occ.shape, BF16),
            pltpu.VMEM(vir.shape, BF16),
            pltpu.VMEM(trial.shape, F32),
            pltpu.VMEM(occ_energy.shape, F32),
            pltpu.VMEM(vir_energy.shape, F32),
            pltpu.SMEM(table.shape, jnp.int32),
            pltpu.VMEM((columns, occupied), F32),
            pltpu.VMEM((kpoints, block, width), F32),
            pltpu.VMEM((vectors, bands * columns, occupied), BF16),
            pltpu.VMEM((bands * columns, rows), BF16),
            pltpu.VMEM((vectors, rows, occupied), BF16),
            pltpu.VMEM((kpoints, vectors * block, occupied), BF16),
            pltpu.VMEM((kpoints, width, occupied), BF16),
            pltpu.VMEM((kpoints, vectors, rows), F32),
            pltpu.VMEM((bands, vectors, rows), F32),
            pltpu.VMEM((rows, 128), F32),
            pltpu.VMEM(coulomb.shape, BF16),
            pltpu.VMEM((kpoints, block, width), BF16),
            pltpu.VMEM((kpoints, vectors * block, width), F32),
            pltpu.VMEM((vectors, groups - 1, 2, block, occupied), F32),
            pltpu.VMEM((vectors, groups, 2, block, occupied), BF16),
            pltpu.VMEM((vectors, 2 * groups + kpoints, block, occupied), BF16),
            pltpu.VMEM((vectors, rows, occupied), BF16),
            pltpu.VMEM((vectors, bands - 1, columns, occupied), BF16),
            pltpu.VMEM((vectors, bands - 1, columns, occupied), BF16),
            dma((8,)),
            dma((vectors + 1,)),
            dma((2, groups)),
            dma((1,)),
            dma((groups, bands - 1)),
            dma((3,)),
            dma((1,)),
            dma((vectors, kpoints)),
            dma((vectors, groups - 2, 2)),
            dma((2,)),
            dma((2,)),
            dma((vectors,)),
            dma((vectors, kpoints + 1)),
            dma((vectors + 1,)),
        ],
        compiler_params=pltpu.CompilerParams(
            collective_id=0, has_side_effects=True, vmem_limit_bytes=56 * 2**20
        ),
        name="coupled",
    )(occ, vir, trial, occ_energy, vir_energy, coulomb, exch, table)


def per_device(
    occ_rows, vir_rows, trial_vectors, occ_energy, vir_energy, coulomb, exch_kernel, minus_table
):
    kpoints = lax.axis_size("ka")
    bands = lax.axis_size("band")
    trial_turned = jnp.swapaxes(trial_vectors[0], 1, 2)
    coupled = coupled_part(
        kpoints,
        bands,
        occ_rows[0],
        vir_rows[0],
        trial_turned,
        occ_energy,
        vir_energy,
        coulomb,
        exch_kernel,
        minus_table,
    )
    return jnp.swapaxes(coupled, 1, 2)[None]


def solution(mesh):
    in_specs = (
        P("ka", "band", None),
        P("ka", "band", None),
        P("ka", None, None, "band"),
        P("ka", None),
        P("ka", "band"),
        P("band", None),
        P(None, "band", None),
        P(),
    )
    out_specs = P("ka", None, None, "band")
    return jax.shard_map(
        per_device, mesh=mesh, in_specs=in_specs, out_specs=out_specs, check_vma=False
    )
```

time: 55.7 us -> 45.7 us (0.82)
  Pallas kernels: 53 us -> 43.9 us
  other arithmetic: 2.48 us -> 0 us
  local copies, waits for them, and re-layouts: 0.01 us -> 1.64 us
    pallas_call x1, Pallas kernels: 53 us -> 43.9 us  [coupled_part(): pl.pallas_call(functools.partial(kernel, kpoints, bands, vectors), out_sh...]
    broadcast_in_dim x1 -> x0, other arithmetic: 1.66 us -> none  [per_device(): return jnp.swapaxes(energy_gaps[None] * trial_turned + coupled, 1, 2)[None]]
    unnamed x2 -> x1, local copies, waits for them, and re-layouts: 0.01 us -> 1.64 us
    sub x1 -> x0, other arithmetic: 0.83 us -> none  [per_device(): energy_gaps = vir_energy[0][:, None] - occ_energy[0][None, :]]
where the time goes in v2:
time: 45.7 us; the launch traced here: 45.5 us
  Pallas kernels  43.9 us (96%)
  local copies, waits for them, and re-layouts  1.64 us (4%)
    pallas_call x1, Pallas kernels, coupled_part(): pl.pallas_call(functools.partial(kernel, kpoints, bands, vectors), out_sh...  43.9 us
    unnamed x1, local copies, waits for them, and re-layouts  1.64 us

profile of v2, /device:TPU:0, one launch (start us, length us, event | category | flops | bytes accessed | tf_op | source)
XLA Modules:
  0.0 45.5 jit_solution(9645579395972843955)
XLA Ops:
  0.0 43.9 %coupled.1 = f32[2,224,128]{2,1,0:T(8,128)} custom-call(bf16[512,128]{1,0:T(8,128)(2,1)} %bitcast.11, bf16[512,896]{1,0:T(8,128)(2,1)} %bitcast.9, f32[2,224,128]{2,1,0:T(8,128)} %bitcast.10, f32[1,128]{1,0:T(1,128)} %occ_energy_given.1, f32[1,224]{1,0:T(1,128)} %vir_energy_given.1, bf16[512,2048]{1,0:T(8,128)(2,1)} %coulomb.1, bf16[8,512,2048]{2,1,0:T(8,128)(2,1)} %exch.1, ...), custom_call_target="tpu_custom_call" | custom-call | tf_op jit(solution)/shard_map/coupled/pallas_call | solution.py:599
  43.9 1.6 %copy.10 = f32[1,2,128,224]{2,3,1,0:T(8,128)} copy(f32[1,2,128,224]{2,3,1,0:T(8,128)} %bitcast.8) | data formatting | bytes 458752

commit v3 on v2

--- a/solution.py
+++ b/solution.py
@@ -59,6 +59,7 @@
     sums_send,
     sums_slot,
     coupling,
+    sigma_own,
     sigma_send,
     sigma_recv,
     local_sem,
@@ -70,6 +71,7 @@
     half_send_sem,
     half_recv_sem,
     half_pass_sem,
+    half_direct_sem,
     dens_sem,
     dens_band_sem,
     sums_send_sem,
@@ -177,6 +179,7 @@
         low = lax.rem(2 * pair + 2 + step, groups)
         high = lax.rem(2 * pair + 2 * groups - 1 - step, groups)
         far_groups.append(lax.select(2 * pair < count, low, high))
+    far_groups.reverse()
     order = [group, partner] + far_groups
 
     mine = tile_of(me)
@@ -260,13 +263,26 @@
                 half_recv_sem.at[v, me],
                 (device, band),
             ).start()
-
-    take_point(partner)
-    for v in range(vectors):
-        own_half(v)
-
-    for source_group in far_groups:
-        take_point(source_group)
+        if v == 0:
+            for copy, direct in direct_copies():
+                pl.when(direct)(copy.start)
+
+    def direct_copies():
+        copies = []
+        for step in range(1, count):
+            other = lax.rem(pair + step, count)
+            above = other > pair
+            distant = lax.select(above, 2 * other + 1, 2 * other)
+            for side_core in range(2):
+                copy = remote(
+                    half_own.at[0, aligned((2 * other + side_core) * block, block)],
+                    half_all.at[me, pl.ds(0, block)],
+                    half_direct_sem.at[step - 1, side_core],
+                    half_recv_sem.at[0, me],
+                    (distant * 2 + side_core, band),
+                )
+                copies.append((copy, lax.select(above, side, 1 - side) == 1))
+        return copies
 
     def half_pass(v, position, owner_core):
         source = far_groups[position] * 2 + owner_core
@@ -283,13 +299,18 @@
         here = half_all.at[source, pl.ds(v * block, block)]
         arrival(here, half_recv_sem.at[v, source]).wait_recv()
 
-    def passing(source_group):
-        return lax.select(source_group < 2 * pair, 1 - side, side) == 1
+    def passing(v, source_group):
+        below = source_group < 2 * pair
+        near = lax.select(below, 1 - side, side)
+        if v:
+            return near == 1
+        source_side = lax.rem(source_group, 2)
+        return near * lax.select(below, 1 - source_side, source_side) == 1
 
     def take_far(v, position):
         for owner_core in range(2):
             take_half(v, far_groups[position] * 2 + owner_core)
-            pl.when(passing(far_groups[position]))(half_pass(v, position, owner_core).start)
+            pl.when(passing(v, far_groups[position]))(half_pass(v, position, owner_core).start)
 
     def occ_turn(position):
         source_group = order[position]
@@ -319,19 +340,24 @@
 
     inner = lax.select(2 * pair < count, side, 1 - side) == 1
 
+    take_point(partner)
+    for v in range(vectors):
+        own_half(v)
+        for source_group in far_groups[v::vectors]:
+            take_point(source_group)
+    for position in range(groups):
+        occ_in(position)
+        if position < groups - 2:
+
+            @pl.when(inner)
+            def _(far=position):
+                take_far(0, far)
+
     @pl.when(inner)
     def _():
-        turns = [(v, far) for v in range(vectors) for far in range(groups - 2)]
-        for position in range(max(groups, len(turns))):
-            if position < groups:
-                occ_in(position)
-            if position < len(turns):
-                take_far(*turns[position])
-
-    @pl.when(jnp.logical_not(inner))
-    def _():
-        for position in range(groups):
-            occ_in(position)
+        for v in range(1, vectors):
+            for far in range(groups - 2):
+                take_far(v, far)
 
     ones = jnp.ones((8, occupied), F32)
     occ_wide = occ[...].astype(F32)
@@ -502,13 +528,6 @@
         sums_slot[v, slot] = totals[1].astype(BF16)
 
 
-    def sigma_of(v, peer):
-        return jnp.dot(
-            vir_turned[aligned(peer * columns, columns), :],
-            coupling[v],
-            preferred_element_type=F32,
-        )
-
     def make_sigma(v):
         drain(sums_slot.at[v, pl.ds(0, 2 * count + 1)], sums_recv_sem.at[v, kpoints])
         for step in range(count):
@@ -521,46 +540,53 @@
                 lines = aligned(which * block, block)
                 direct = 2.0 * potential[lines, v : v + 1] * occ[lines, :].astype(F32)
                 coupling[v, lines, :] = (direct - total).astype(BF16)
+        total = jnp.dot(vir_turned[...], coupling[v], preferred_element_type=F32)
+        sigma_own[...] = total
+        sigma_send[v] = total.astype(BF16)
         for way, peer in enumerate(others):
-            sigma_send[v, way] = sigma_of(v, peer).astype(BF16)
             remote(
-                sigma_send.at[v, way],
+                sigma_send.at[v, pl.ds(pl.multiple_of(peer * columns, 16), columns)],
                 sigma_recv.at[v, way],
                 sigma_sem.at[vectors],
                 sigma_sem.at[v],
                 (me, peer),
             ).start()
-        out[v] = gaps[...] * trial[v] + sigma_of(v, band)
+        out[v] = gaps[...] * trial[v] + sigma_own[pl.ds(pl.multiple_of(band * columns, 16), columns)]
 
     take_halves(0)
-    for position in range(groups // 2):
-        take_corner(position)
     drain(occ_tile.at[pl.ds(0, groups), pl.ds(0, width - piece)], occ_pass_sem.at[1])
     make_pairs(0, (band, near_x, near_y))
-    screen_far(0, 0, early)
-    for position in range(groups // 2, groups):
+    for step in range(groups - 2):
+        take_corner(step)
+        screen_far(0, step, early)
+    for position in range(groups - 2, groups):
         take_corner(position)
     drain(occ_tile.at[pl.ds(0, groups), pl.ds(0, piece)], occ_pass_sem.at[2])
     make_pairs(0, (corner,))
-    screen_far(0, 0, late, True)
-    send_far(0, 0)
-    for step in range(1, groups - 1):
-        screen_far(0, step, whole)
+    for step in range(groups - 2):
+        screen_far(0, step, late, True)
         send_far(0, step)
+
+    def both_far(v, step):
+        screen_far(v, step, whole)
+        send_far(v, step)
+
     sum_density()
     for v in range(1, vectors):
         take_halves(v)
         make_pairs(v, (band, near_x, near_y, corner))
-        for step in range(groups - 1):
-            screen_far(v, step, whole)
-            send_far(v, step)
-        gather_far(v - 1)
+        for step in range(groups - 2):
+            both_far(v, step)
+    for v in range(vectors):
+        both_far(v, groups - 2)
+        if v == 0:
+            gather_far(0)
     send_own(0)
+    for v in range(1, vectors):
+        gather_far(v)
+        send_own(v)
     make_potential()
-    gather_far(vectors - 1)
-    make_sigma(0)
-    for v in range(1, vectors):
-        send_own(v)
+    for v in range(vectors):
         make_sigma(v)
     for v in range(vectors):
         drain(sigma_recv.at[v], sigma_sem.at[v])
@@ -569,8 +595,8 @@
             result += sigma_recv[v, way].astype(F32)
         out[v] = result
 
-    drain(sigma_send, trial_sem.at[vectors])
-    drain(sigma_send, sigma_sem.at[vectors])
+    drain(sigma_recv, trial_sem.at[vectors])
+    drain(sigma_recv, sigma_sem.at[vectors])
     for copy in point_copies:
         copy.wait_send()
     drain(occ_tile.at[pl.ds(0, groups), pl.ds(0, width - piece)], occ_send_sem.at[0])
@@ -582,7 +608,9 @@
         drain(sums_slot.at[v, pl.ds(0, 2 * groups - 1)], sums_send_sem.at[v])
         for far in range(groups - 2):
             for owner_core in range(2):
-                pl.when(passing(far_groups[far]))(half_pass(v, far, owner_core).wait_send)
+                pl.when(passing(v, far_groups[far]))(half_pass(v, far, owner_core).wait_send)
+    for copy, direct in direct_copies():
+        pl.when(direct)(copy.wait_send)
 
 
 def coupled_part(
@@ -591,6 +619,7 @@
     rows, occupied = occ.shape
     vectors, columns = trial.shape[:2]
     groups = kpoints // 2
+    count = groups // 2
     block = rows // groups
     width = bands * rows // 2
     vmem = pl.BlockSpec(memory_space=pltpu.VMEM)
@@ -598,7 +627,7 @@
     dma = pltpu.SemaphoreType.DMA
     return pl.pallas_call(
         functools.partial(kernel, kpoints, bands, vectors),
-        out_shape=jax.ShapeDtypeStruct(trial.shape, F32),
+        out_shape=pltpu.VMEM(trial.shape, F32),
         in_specs=[hbm] * 8,
         out_specs=vmem,
         scratch_shapes=[
@@ -625,7 +654,8 @@
             pltpu.VMEM((vectors, groups, 2, block, occupied), BF16),
             pltpu.VMEM((vectors, 2 * groups + kpoints, block, occupied), BF16),
             pltpu.VMEM((vectors, rows, occupied), BF16),
-            pltpu.VMEM((vectors, bands - 1, columns, occupied), BF16),
+            pltpu.VMEM((bands * columns, occupied), F32),
+            pltpu.VMEM((vectors, bands * columns, occupied), BF16),
             pltpu.VMEM((vectors, bands - 1, columns, occupied), BF16),
             dma((8,)),
             dma((vectors + 1,)),
@@ -636,6 +666,7 @@
             dma((1,)),
             dma((vectors, kpoints)),
             dma((vectors, groups - 2, 2)),
+            dma((count - 1, 2)),
             dma((2,)),
             dma((2,)),
             dma((vectors,)),
@@ -643,10 +674,15 @@
             dma((vectors + 1,)),
         ],
         compiler_params=pltpu.CompilerParams(
-            collective_id=0, has_side_effects=True, vmem_limit_bytes=56 * 2**20
+            collective_id=0, has_side_effects=True, vmem_limit_bytes=40 * 2**20
         ),
         name="coupled",
-    )(occ, vir, trial, occ_energy, vir_energy, coulomb, exch, table)
+    )(
+        *(
+            pltpu.with_memory_space_constraint(given, pltpu.HBM)
+            for given in (occ, vir, trial, occ_energy, vir_energy, coulomb, exch, table)
+        )
+    )
 
 
 def per_device(

time: 45.7 us -> 42.9 us (0.939)
  Pallas kernels: 43.9 us -> 42 us
  local copies, waits for them, and re-layouts: 1.64 us -> 0.69 us
    pallas_call x1, Pallas kernels: 43.9 us -> 42 us  [coupled_part(): pl.pallas_call(functools.partial(kernel, kpoints, bands, vectors), out_sh...]
    unnamed x1, local copies, waits for them, and re-layouts: 1.64 us -> 0.69 us
where the time goes in v3:
time: 42.9 us; the launch traced here: 42.7 us
  Pallas kernels  42 us (98%)
  local copies, waits for them, and re-layouts  0.69 us (2%)
    pallas_call x1, Pallas kernels, coupled_part(): pl.pallas_call(functools.partial(kernel, kpoints, bands, vectors), out_sh...  42 us

profile of v3, /device:TPU:0, one launch (start us, length us, event | category | flops | bytes accessed | tf_op | source)
XLA Modules:
  0.0 42.7 jit_solution(13054118034302701258)
XLA Ops:
  0.0 42.0 %coupled.1 = f32[2,224,128]{2,1,0:T(8,128)S(1)} custom-call(bf16[512,128]{1,0:T(8,128)(2,1)} %bitcast.11, bf16[512,896]{1,0:T(8,128)(2,1)} %bitcast.9, f32[2,224,128]{2,1,0:T(8,128)} %bitcast.10, f32[1,128]{1,0:T(1,128)} %occ_energy_given.1, f32[1,224]{1,0:T(1,128)} %vir_energy_given.1, bf16[512,2048]{1,0:T(8,128)(2,1)} %coulomb.1, ...), custom_call_target="tpu_custom_call" | custom-call | tf_op jit(solution)/shard_map/coupled/pallas_call | solution.py:628
  42.0 0.7 %copy.10 = f32[1,2,128,224]{2,3,1,0:T(8,128)} copy(f32[1,2,128,224]{2,3,1,0:T(8,128)S(1)} %bitcast.8) | data formatting | bytes 458752

commit v4 on v3

--- a/solution.py
+++ b/solution.py
@@ -353,12 +353,6 @@
             def _(far=position):
                 take_far(0, far)
 
-    @pl.when(inner)
-    def _():
-        for v in range(1, vectors):
-            for far in range(groups - 2):
-                take_far(v, far)
-
     ones = jnp.ones((8, occupied), F32)
     occ_wide = occ[...].astype(F32)
     dens_all[me] = jnp.concatenate(
@@ -376,6 +370,12 @@
             dens_sem.at[1],
             (lax.rem(me + step, kpoints), band),
         ).start()
+
+    @pl.when(inner)
+    def _():
+        for v in range(1, vectors):
+            for far in range(groups - 2):
+                take_far(v, far)
 
     def take_corner(position):
         source_group = order[position]
@@ -500,18 +500,16 @@
                     lax.select(through, target, kpoints),
                 )
 
-    def gather_far(v):
-        for step in range(groups - 1):
-
-            @pl.when(step > outward)
-            def _(step=step):
-                for n in range(2):
-                    target = far_target(step) * 2 + n
-                    before = sums_slot.at[v, 2 * groups + target]
-                    arrival(before, sums_recv_sem.at[v, target]).wait_recv()
-                    total = held[v, step, n] + before[...].astype(F32)
-                    sums_send[v, step, n] = total.astype(BF16)
-                    sums_to(v, step, n, target, 2 * own_block, kpoints)
+    def gather_far(v, step):
+        @pl.when(step > outward)
+        def _():
+            for n in range(2):
+                target = far_target(step) * 2 + n
+                before = sums_slot.at[v, 2 * groups + target]
+                arrival(before, sums_recv_sem.at[v, target]).wait_recv()
+                total = held[v, step, n] + before[...].astype(F32)
+                sums_send[v, step, n] = total.astype(BF16)
+                sums_to(v, step, n, target, 2 * own_block, kpoints)
 
     def send_own(v):
         totals = screen(v, [sibling, me], whole)
@@ -558,9 +556,10 @@
     make_pairs(0, (band, near_x, near_y))
     for step in range(groups - 2):
         take_corner(step)
+        if step == groups - 3:
+            for position in range(groups - 2, groups):
+                take_corner(position)
         screen_far(0, step, early)
-    for position in range(groups - 2, groups):
-        take_corner(position)
     drain(occ_tile.at[pl.ds(0, groups), pl.ds(0, piece)], occ_pass_sem.at[2])
     make_pairs(0, (corner,))
     for step in range(groups - 2):
@@ -577,16 +576,20 @@
         make_pairs(v, (band, near_x, near_y, corner))
         for step in range(groups - 2):
             both_far(v, step)
+    for step in range(groups - 2):
+        gather_far(0, step)
+    both_far(0, groups - 2)
+    gather_far(0, groups - 2)
+    for v in range(1, vectors):
+        both_far(v, groups - 2)
+        for step in range(groups - 2):
+            gather_far(v, step)
     for v in range(vectors):
-        both_far(v, groups - 2)
+        send_own(v)
         if v == 0:
-            gather_far(0)
-    send_own(0)
-    for v in range(1, vectors):
-        gather_far(v)
-        send_own(v)
-    make_potential()
-    for v in range(vectors):
+            for later in range(1, vectors):
+                gather_far(later, groups - 2)
+            make_potential()
         make_sigma(v)
     for v in range(vectors):
         drain(sigma_recv.at[v], sigma_sem.at[v])

time: 42.9 us -> 41.2 us (0.960)
  Pallas kernels: 42 us -> 40.3 us
    pallas_call x1, Pallas kernels: 42 us -> 40.3 us  [coupled_part(): pl.pallas_call(functools.partial(kernel, kpoints, bands, vectors), out_sh...]
where the time goes in v4:
time: 41.2 us; the launch traced here: 41 us
  Pallas kernels  40.3 us (98%)
  local copies, waits for them, and re-layouts  0.69 us (2%)
    pallas_call x1, Pallas kernels, coupled_part(): pl.pallas_call(functools.partial(kernel, kpoints, bands, vectors), out_sh...  40.3 us

profile of v4, /device:TPU:0, one launch (start us, length us, event | category | flops | bytes accessed | tf_op | source)
XLA Modules:
  0.0 41.0 jit_solution(6552437344695208728)
XLA Ops:
  0.0 40.3 %coupled.1 = f32[2,224,128]{2,1,0:T(8,128)S(1)} custom-call(bf16[512,128]{1,0:T(8,128)(2,1)} %bitcast.11, bf16[512,896]{1,0:T(8,128)(2,1)} %bitcast.9, f32[2,224,128]{2,1,0:T(8,128)} %bitcast.10, f32[1,128]{1,0:T(1,128)} %occ_energy_given.1, f32[1,224]{1,0:T(1,128)} %vir_energy_given.1, bf16[512,2048]{1,0:T(8,128)(2,1)} %coulomb.1, ...), custom_call_target="tpu_custom_call" | custom-call | tf_op jit(solution)/shard_map/coupled/pallas_call | solution.py:631
  40.3 0.7 %copy.10 = f32[1,2,128,224]{2,3,1,0:T(8,128)} copy(f32[1,2,128,224]{2,3,1,0:T(8,128)S(1)} %bitcast.8) | data formatting | bytes 458752

commit v5 on v4

--- a/solution.py
+++ b/solution.py
@@ -101,6 +101,9 @@
     def tile_of(k):
         return lax.rem(k, 2) * groups + lax.div(k, 2)
 
+    def rank(k, home):
+        return lax.select(k < 4 * home, k, k - 4)
+
     def remote(source, target, send, recv, device):
         return pltpu.make_async_remote_copy(
             src_ref=source,
@@ -184,17 +187,15 @@
 
     mine = tile_of(me)
     occ_load.wait()
-    point_copies = []
-    for step, peer in enumerate(order[1:]):
+    for peer in order[1:]:
         copy = remote(
             occ.at[aligned(lax.rem(peer, 2) * piece, piece)],
             occ_tile.at[mine, piece_of(band)],
-            point_sem.at[0, step],
-            point_sem.at[1, group],
+            point_sem.at[groups],
+            point_sem.at[group],
             (peer * 2 + core, band),
         )
         copy.start()
-        point_copies.append(copy)
     occ_tile[mine, piece_of(band), :] = occ[aligned(side * piece, piece), :]
 
     def occ_out(source_group):
@@ -205,7 +206,7 @@
                 here,
                 here,
                 occ_send_sem.at[0],
-                occ_sem.at[source_group, way - 1],
+                occ_sem.at[source_group, 0],
                 (me, peer),
             ).start()
         occ_pass(source_group, 0, band).start()
@@ -238,7 +239,7 @@
     def take_point(source_group):
         arrival(
             occ_tile.at[core * groups + source_group, piece_of(band)],
-            point_sem.at[1, source_group],
+            point_sem.at[source_group],
         ).wait_recv()
         occ_out(source_group)
 
@@ -252,15 +253,20 @@
         for step in range(1, count):
             other = lax.rem(pair + step, count)
             near = lax.select(other > pair, 2 * other, 2 * other + 1)
-            destinations += [(2 * other + side_core, near * 2 + side_core) for side_core in range(2)]
-        destinations += [(2 * pair + side_core, partner * 2 + side_core) for side_core in range(2)]
-        destinations.append((2 * pair + 1 - core, sibling))
-        for which, device in destinations:
+            destinations += [
+                (2 * other + side_core, near * 2 + side_core, rank(me, other))
+                for side_core in range(2)
+            ]
+        destinations += [
+            (2 * pair + side_core, partner * 2 + side_core, kpoints - 4) for side_core in range(2)
+        ]
+        destinations.append((2 * pair + 1 - core, sibling, kpoints - 4))
+        for which, device, slot in destinations:
             remote(
                 half_own.at[v, aligned(which * block, block)],
                 half_all.at[me, lines],
                 half_send_sem.at[0],
-                half_recv_sem.at[v, me],
+                half_recv_sem.at[v, slot],
                 (device, band),
             ).start()
         if v == 0:
@@ -278,7 +284,7 @@
                     half_own.at[0, aligned((2 * other + side_core) * block, block)],
                     half_all.at[me, pl.ds(0, block)],
                     half_direct_sem.at[step - 1, side_core],
-                    half_recv_sem.at[0, me],
+                    half_recv_sem.at[0, rank(me, other)],
                     (distant * 2 + side_core, band),
                 )
                 copies.append((copy, lax.select(above, side, 1 - side) == 1))
@@ -291,13 +297,13 @@
             here,
             here,
             half_pass_sem.at[v, position, owner_core],
-            half_recv_sem.at[v, source],
+            half_recv_sem.at[v, rank(source, pair)],
             (partner * 2 + core, band),
         )
 
     def take_half(v, source):
         here = half_all.at[source, pl.ds(v * block, block)]
-        arrival(here, half_recv_sem.at[v, source]).wait_recv()
+        arrival(here, half_recv_sem.at[v, rank(source, pair)]).wait_recv()
 
     def passing(v, source_group):
         below = source_group < 2 * pair
@@ -324,18 +330,16 @@
             here,
             here,
             occ_send_sem.at[0],
-            occ_sem.at[source_group, 2],
+            occ_sem.at[source_group, 1],
             (me, onward),
         )
 
     def occ_in(position):
         source_group = order[position]
         tile = core * groups + source_group
+        drain(occ_tile.at[tile, pl.ds(0, 2 * piece)], occ_sem.at[source_group, 0])
+        occ_turn(position).start()
         for way, owner in ((1, near_x), (2, near_y)):
-            here = occ_tile.at[tile, piece_of(owner)]
-            arrival(here, occ_sem.at[source_group, way - 1]).wait_recv()
-            if (position < groups // 2) == (way == 1):
-                occ_turn(position).start()
             occ_pass(source_group, way, owner).start()
 
     inner = lax.select(2 * pair < count, side, 1 - side) == 1
@@ -380,13 +384,11 @@
     def take_corner(position):
         source_group = order[position]
         here = occ_tile.at[core * groups + source_group, piece_of(corner)]
-        arrival(here, occ_sem.at[source_group, 2]).wait_recv()
+        arrival(here, occ_sem.at[source_group, 1]).wait_recv()
         occ_pass(source_group, bands - 1, corner).start()
 
     def take_halves(v):
-        take_half(v, sibling)
-        for source in (partner * 2, partner * 2 + 1):
-            take_half(v, source)
+        drain(half_all.at[pl.ds(0, 3), pl.ds(v * block, block)], half_recv_sem.at[v, kpoints - 4])
 
         @pl.when(jnp.logical_not(inner))
         def _():
@@ -497,7 +499,7 @@
                     n,
                     lax.select(through, partner * 2 + core, target),
                     lax.select(through, 2 * groups + target, 2 * own_block + side),
-                    lax.select(through, target, kpoints),
+                    lax.select(through, rank(target, pair), kpoints - 4),
                 )
 
     def gather_far(v, step):
@@ -506,10 +508,10 @@
             for n in range(2):
                 target = far_target(step) * 2 + n
                 before = sums_slot.at[v, 2 * groups + target]
-                arrival(before, sums_recv_sem.at[v, target]).wait_recv()
+                arrival(before, sums_recv_sem.at[v, rank(target, pair)]).wait_recv()
                 total = held[v, step, n] + before[...].astype(F32)
                 sums_send[v, step, n] = total.astype(BF16)
-                sums_to(v, step, n, target, 2 * own_block, kpoints)
+                sums_to(v, step, n, target, 2 * own_block, kpoints - 4)
 
     def send_own(v):
         totals = screen(v, [sibling, me], whole)
@@ -520,14 +522,14 @@
             sending,
             sums_slot.at[v, slot],
             sums_send_sem.at[v],
-            sums_recv_sem.at[v, kpoints],
+            sums_recv_sem.at[v, kpoints - 4],
             (sibling, band),
         ).start()
         sums_slot[v, slot] = totals[1].astype(BF16)
 
 
     def make_sigma(v):
-        drain(sums_slot.at[v, pl.ds(0, 2 * count + 1)], sums_recv_sem.at[v, kpoints])
+        drain(sums_slot.at[v, pl.ds(0, 2 * count + 1)], sums_recv_sem.at[v, kpoints - 4])
         for step in range(count):
             other = lax.rem(pair + step, count)
             for side_core in range(2):
@@ -600,8 +602,9 @@
 
     drain(sigma_recv, trial_sem.at[vectors])
     drain(sigma_recv, sigma_sem.at[vectors])
-    for copy in point_copies:
-        copy.wait_send()
+    drain(
+        exch_tile.at[pl.ds(0, groups - 1), pl.ds(0, occupied // bands)], point_sem.at[groups]
+    )
     drain(occ_tile.at[pl.ds(0, groups), pl.ds(0, width - piece)], occ_send_sem.at[0])
     drain(occ_tile.at[pl.ds(0, groups)], occ_pass_sem.at[0])
     drain(half_all.at[pl.ds(0, groups + 1)], half_send_sem.at[0])
@@ -662,18 +665,18 @@
             pltpu.VMEM((vectors, bands - 1, columns, occupied), BF16),
             dma((8,)),
             dma((vectors + 1,)),
-            dma((2, groups)),
+            dma((groups + 1,)),
             dma((1,)),
-            dma((groups, bands - 1)),
+            dma((groups, 2)),
             dma((3,)),
             dma((1,)),
-            dma((vectors, kpoints)),
+            dma((vectors, kpoints - 3)),
             dma((vectors, groups - 2, 2)),
             dma((count - 1, 2)),
             dma((2,)),
             dma((2,)),
             dma((vectors,)),
-            dma((vectors, kpoints + 1)),
+            dma((vectors, kpoints - 3)),
             dma((vectors + 1,)),
         ],
         compiler_params=pltpu.CompilerParams(

time: 41.2 us -> 41 us (level)
  no operation moved by 1% of the time
where the time goes in v5:
time: 41 us; the launch traced here: 40.8 us
  Pallas kernels  40.1 us (98%)
  local copies, waits for them, and re-layouts  0.69 us (2%)
    pallas_call x1, Pallas kernels, coupled_part(): pl.pallas_call(functools.partial(kernel, kpoints, bands, vectors), out_sh...  40.1 us

profile of v5, /device:TPU:0, one launch (start us, length us, event | category | flops | bytes accessed | tf_op | source)
XLA Modules:
  0.0 40.8 jit_solution(16199844861755284032)
XLA Ops:
  0.0 40.1 %coupled.1 = f32[2,224,128]{2,1,0:T(8,128)S(1)} custom-call(bf16[512,128]{1,0:T(8,128)(2,1)} %bitcast.11, bf16[512,896]{1,0:T(8,128)(2,1)} %bitcast.9, f32[2,224,128]{2,1,0:T(8,128)} %bitcast.10, f32[1,128]{1,0:T(1,128)} %occ_energy_given.1, f32[1,224]{1,0:T(1,128)} %vir_energy_given.1, bf16[512,2048]{1,0:T(8,128)(2,1)} %coulomb.1, ...), custom_call_target="tpu_custom_call" | custom-call | tf_op jit(solution)/shard_map/coupled/pallas_call | solution.py:634
  40.1 0.7 %copy.10 = f32[1,2,128,224]{2,3,1,0:T(8,128)} copy(f32[1,2,128,224]{2,3,1,0:T(8,128)S(1)} %bitcast.8) | data formatting | bytes 458752

commit v6 on v5

--- a/solution.py
+++ b/solution.py
@@ -117,6 +117,9 @@
     def arrival(target, recv):
         return remote(target, target, recv, recv, (sibling, band))
 
+    def piece_at(way):
+        return pl.ds(way * piece, piece)
+
     def drain(held, sem):
         pltpu.make_async_copy(held, held, sem).wait()
 
@@ -146,14 +149,14 @@
         copy.start()
         load_copies.append(copy)
     trial_load, occ_load, vir_load, *other_loads = load_copies
-    for part in range(bands):
+    for way, owner in enumerate((band, near_x, near_y, corner)):
         pltpu.make_async_copy(
             exch.at[
                 :,
                 aligned((2 * pair + core) * block, block),
-                aligned(part * rows + side * piece, piece),
+                aligned(owner * rows + side * piece, piece),
             ],
-            exch_tile.at[:, :, pl.ds(part * piece, piece)],
+            exch_tile.at[:, :, piece_at(way)],
             local_sem.at[1],
         ).start()
     coulomb_copy = pltpu.make_async_copy(coulomb, coulomb_here, local_sem.at[0])
@@ -174,9 +177,6 @@
                 (me, peer),
             ).start()
 
-    def piece_of(owner):
-        return aligned(owner * piece, piece)
-
     far_groups = []
     for step in range(groups - 2):
         low = lax.rem(2 * pair + 2 + step, groups)
@@ -190,29 +190,29 @@
     for peer in order[1:]:
         copy = remote(
             occ.at[aligned(lax.rem(peer, 2) * piece, piece)],
-            occ_tile.at[mine, piece_of(band)],
+            occ_tile.at[mine, piece_at(0)],
             point_sem.at[groups],
             point_sem.at[group],
             (peer * 2 + core, band),
         )
         copy.start()
-    occ_tile[mine, piece_of(band), :] = occ[aligned(side * piece, piece), :]
+    occ_tile[mine, piece_at(0), :] = occ[aligned(side * piece, piece), :]
 
     def occ_out(source_group):
         tile = core * groups + source_group
-        here = occ_tile.at[tile, piece_of(band)]
+        here = occ_tile.at[tile, piece_at(0)]
         for way, peer in ((1, near_x), (2, near_y)):
             remote(
                 here,
-                here,
+                occ_tile.at[tile, piece_at(way)],
                 occ_send_sem.at[0],
                 occ_sem.at[source_group, 0],
                 (me, peer),
             ).start()
-        occ_pass(source_group, 0, band).start()
-
-    def occ_pass(source_group, way, owner):
-        here = occ_tile.at[core * groups + source_group, piece_of(owner)]
+        occ_pass(source_group, 0).start()
+
+    def occ_pass(source_group, way, pieces=1):
+        here = occ_tile.at[core * groups + source_group, pl.ds(way * piece, pieces * piece)]
         return remote(
             here,
             here,
@@ -238,7 +238,7 @@
 
     def take_point(source_group):
         arrival(
-            occ_tile.at[core * groups + source_group, piece_of(band)],
+            occ_tile.at[core * groups + source_group, piece_at(0)],
             point_sem.at[source_group],
         ).wait_recv()
         occ_out(source_group)
@@ -321,14 +321,10 @@
     def occ_turn(position):
         source_group = order[position]
         tile = core * groups + source_group
-        if position < groups // 2:
-            owner, onward = near_x, near_y
-        else:
-            owner, onward = near_y, near_x
-        here = occ_tile.at[tile, piece_of(owner)]
+        way, onward = (1, near_y) if position < groups // 2 else (2, near_x)
         return remote(
-            here,
-            here,
+            occ_tile.at[tile, piece_at(way)],
+            occ_tile.at[tile, piece_at(bands - 1)],
             occ_send_sem.at[0],
             occ_sem.at[source_group, 1],
             (me, onward),
@@ -339,8 +335,7 @@
         tile = core * groups + source_group
         drain(occ_tile.at[tile, pl.ds(0, 2 * piece)], occ_sem.at[source_group, 0])
         occ_turn(position).start()
-        for way, owner in ((1, near_x), (2, near_y)):
-            occ_pass(source_group, way, owner).start()
+        occ_pass(source_group, 1, 2).start()
 
     inner = lax.select(2 * pair < count, side, 1 - side) == 1
 
@@ -383,9 +378,9 @@
 
     def take_corner(position):
         source_group = order[position]
-        here = occ_tile.at[core * groups + source_group, piece_of(corner)]
+        here = occ_tile.at[core * groups + source_group, piece_at(bands - 1)]
         arrival(here, occ_sem.at[source_group, 1]).wait_recv()
-        occ_pass(source_group, bands - 1, corner).start()
+        occ_pass(source_group, bands - 1).start()
 
     def take_halves(v):
         drain(half_all.at[pl.ds(0, 3), pl.ds(v * block, block)], half_recv_sem.at[v, kpoints - 4])
@@ -395,18 +390,12 @@
             for far in range(groups - 2):
                 take_far(v, far)
 
-    def make_pairs(v, owners):
-        lines = pl.ds(v * block, block)
+    def make_pairs(v, first, size):
+        lines, part = pl.ds(v * block, block), pl.ds(first, size)
         for source in range(kpoints):
-            tile = tile_of(source)
-            if len(owners) == bands:
-                pairs[source, lines] = dot_nt(half_all[source, lines], occ_tile[tile])
-                continue
-            for owner in owners:
-                part = piece_of(owner)
-                pairs[source, lines, part] = dot_nt(
-                    half_all[source, lines], occ_tile[tile, part]
-                )
+            pairs[source, lines, part] = dot_nt(
+                half_all[source, lines], occ_tile[tile_of(source), part]
+            )
 
     def sum_density():
         drain(dens_all.at[pl.ds(0, kpoints - 1)], dens_sem.at[1])
@@ -433,10 +422,10 @@
             total += dot_nt(coulomb_here[:, part * rows : (part + 1) * rows], here)
         potential[:, :16] = total
 
-    def screen(v, targets, spans):
+    def screen(v, targets, parts):
         sources = [[table[target, q] for q in range(kpoints)] for target in targets]
         results = [jnp.zeros((block, occupied), F32) for _ in targets]
-        for across, span in spans:
+        for across, span in parts:
             chunks = [[] for _ in targets]
             for start in range(0, block, CHUNK):
                 totals = [jnp.zeros((CHUNK, span), F32) for _ in targets]
@@ -455,9 +444,13 @@
                 )
         return results
 
-    whole = [(pl.ds(first, SPAN), SPAN) for first in range(0, width, SPAN)]
-    early = [(piece_of(owner), piece) for owner in (band, near_x, near_y)]
-    late = [(piece_of(corner), piece)]
+    def spans(first, last):
+        starts = range(first, last, SPAN)
+        return [(pl.ds(start, min(SPAN, last - start)), min(SPAN, last - start)) for start in starts]
+
+    whole = spans(0, width)
+    early = spans(0, width - piece)
+    late = spans(width - piece, width)
 
     own_block = 2 * pair + core
     lower = 2 * pair
@@ -478,9 +471,9 @@
             (device, band),
         ).start()
 
-    def screen_far(v, step, spans, before=None):
+    def screen_far(v, step, parts, before=None):
         target_group = far_target(step)
-        totals = screen(v, [target_group * 2 + n for n in range(2)], spans)
+        totals = screen(v, [target_group * 2 + n for n in range(2)], parts)
         for n in range(2):
             held[v, step, n] = totals[n] if before is None else held[v, step, n] + totals[n]
 
@@ -555,7 +548,7 @@
 
     take_halves(0)
     drain(occ_tile.at[pl.ds(0, groups), pl.ds(0, width - piece)], occ_pass_sem.at[1])
-    make_pairs(0, (band, near_x, near_y))
+    make_pairs(0, 0, width - piece)
     for step in range(groups - 2):
         take_corner(step)
         if step == groups - 3:
@@ -563,7 +556,7 @@
                 take_corner(position)
         screen_far(0, step, early)
     drain(occ_tile.at[pl.ds(0, groups), pl.ds(0, piece)], occ_pass_sem.at[2])
-    make_pairs(0, (corner,))
+    make_pairs(0, width - piece, piece)
     for step in range(groups - 2):
         screen_far(0, step, late, True)
         send_far(0, step)
@@ -575,7 +568,7 @@
     sum_density()
     for v in range(1, vectors):
         take_halves(v)
-        make_pairs(v, (band, near_x, near_y, corner))
+        make_pairs(v, 0, width)
         for step in range(groups - 2):
             both_far(v, step)
     for step in range(groups - 2):

time: 41 us -> 40.9 us (level)
  no operation moved by 1% of the time
where the time goes in v6:
time: 40.9 us; the launch traced here: 40.7 us
  Pallas kernels  40 us (98%)
  local copies, waits for them, and re-layouts  0.69 us (2%)
    pallas_call x1, Pallas kernels, coupled_part(): pl.pallas_call(functools.partial(kernel, kpoints, bands, vectors), out_sh...  40 us

profile of v6, /device:TPU:0, one launch (start us, length us, event | category | flops | bytes accessed | tf_op | source)
XLA Modules:
  0.0 40.7 jit_solution(9619023314635609540)
XLA Ops:
  0.0 40.0 %coupled.1 = f32[2,224,128]{2,1,0:T(8,128)S(1)} custom-call(bf16[512,128]{1,0:T(8,128)(2,1)} %bitcast.11, bf16[512,896]{1,0:T(8,128)(2,1)} %bitcast.9, f32[2,224,128]{2,1,0:T(8,128)} %bitcast.10, f32[1,128]{1,0:T(1,128)} %occ_energy_given.1, f32[1,224]{1,0:T(1,128)} %vir_energy_given.1, bf16[512,2048]{1,0:T(8,128)(2,1)} %coulomb.1, ...), custom_call_target="tpu_custom_call" | custom-call | tf_op jit(solution)/shard_map/coupled/pallas_call | solution.py:627
  40.0 0.7 %copy.10 = f32[1,2,128,224]{2,3,1,0:T(8,128)} copy(f32[1,2,128,224]{2,3,1,0:T(8,128)S(1)} %bitcast.8) | data formatting | bytes 458752
